TPU v7x, 128 devices: a whole 4x4x4 slice. The times are simulated.
128 devices in a mesh: datb: 4 (over z), model: 4 (over y), data: 8 (over x, core).
Axes of the slice: x: 4, y: 4, z: 4, core: 2. Of those that a mesh axis runs over, the one named last changes fastest.
Arguments:
- tokens: bfloat16 [8192, 3584], P(('datb', 'data', 'model'))
- w_gate: bfloat16 [3584, 18944], P(('datb', 'data'), 'model')
- w_up: bfloat16 [3584, 18944], P(('datb', 'data'), 'model')
- w_down: bfloat16 [18944, 3584], P('model', ('datb', 'data'))
- grad_out: bfloat16 [8192, 3584], P(('datb', 'data', 'model'))
Outputs:
- output 1: bfloat16 [8192, 3584], P(('datb', 'data', 'model'))
- output 2: bfloat16 [8192, 3584], P(('datb', 'data', 'model'))
- output 3: float32 [3584, 18944], P(('datb', 'data'), 'model')
- output 4: float32 [3584, 18944], P(('datb', 'data'), 'model')
- output 5: float32 [18944, 3584], P('model', ('datb', 'data'))
All inputs are finite; a program needn't handle non-finite values.
Results may differ from a plain program's by a relative error of at most 0.02.
Values are sent between devices in bfloat16 or wider.
A program may use at most 1 GiB of HBM per device.

v0:
```python
import jax
import jax.numpy as jnp
from jax import lax
from jax.sharding import PartitionSpec as P

ROW_SPEC = P(("datb", "data", "model"), None)
GATE_SPEC = P(("datb", "data"), "model")
DOWN_SPEC = P("model", ("datb", "data"))


def solution(mesh):
    datb_size = mesh.shape["datb"]
    data_size = mesh.shape["data"]
    model_size = mesh.shape["model"]

    def local_step(tok_loc, wg_loc, wu_loc, wd_loc, grad_loc):
        rows_dev, d_model = tok_loc.shape
        d_part = wg_loc.shape[0]
        shard_rows = rows_dev * model_size

        def to_rows(part_out):
            per_model = lax.psum_scatter(part_out.reshape(data_size, model_size, rows_dev, datb_size, d_part), "model", scatter_dimension=1)
            moved_rows = lax.all_to_all(per_model[:, :, :, None, :], "data", 0, 3, tiled=True)
            return moved_rows.reshape(rows_dev, d_model)

        gate_w = lax.all_gather(wg_loc, "datb", axis=0)
        up_w = lax.all_gather(wu_loc, "datb", axis=0)
        down_w = lax.all_gather(wd_loc, "datb", axis=1)

        tok_full = lax.all_gather(tok_loc, "model", axis=0, tiled=True)
        tok_split = lax.all_to_all(tok_full.reshape(shard_rows, datb_size, data_size, d_part), "data", 2, 2, tiled=True)
        gate_part = jnp.einsum("tbae,bef->taf", tok_split, gate_w, preferred_element_type=jnp.float32).astype(jnp.bfloat16)
        up_part = jnp.einsum("tbae,bef->taf", tok_split, up_w, preferred_element_type=jnp.float32).astype(jnp.bfloat16)
        gate_pre = lax.psum_scatter(gate_part, "data", scatter_dimension=1).astype(jnp.float32)
        up_pre = lax.psum_scatter(up_part, "data", scatter_dimension=1).astype(jnp.float32)
        gate_sig = jax.nn.sigmoid(gate_pre)
        silu_gate = gate_pre * gate_sig
        hidden = (silu_gate * up_pre).astype(jnp.bfloat16)
        hid_all = lax.all_gather(hidden, "data", axis=0)
        down_part = jnp.einsum("atf,fbe->atbe", hid_all, down_w, preferred_element_type=jnp.float32).astype(jnp.bfloat16)
        out = (tok_loc.astype(jnp.float32) + to_rows(down_part).astype(jnp.float32)).astype(jnp.bfloat16)

        grad_full = lax.all_gather(grad_loc, "model", axis=0, tiled=True)
        grad_split = lax.all_to_all(grad_full.reshape(shard_rows, datb_size, data_size, d_part), "data", 2, 2, tiled=True)
        grad_hid_part = jnp.einsum("tbae,fbe->taf", grad_split, down_w, preferred_element_type=jnp.float32).astype(jnp.bfloat16)
        grad_hidden = lax.psum_scatter(grad_hid_part, "data", scatter_dimension=1).astype(jnp.float32)
        grad_gate_pre = (grad_hidden * up_pre * gate_sig * (1.0 + gate_pre * (1.0 - gate_sig))).astype(jnp.bfloat16)
        grad_up_pre = (grad_hidden * silu_gate).astype(jnp.bfloat16)
        dgate_all = lax.all_gather(grad_gate_pre, "data", axis=0)
        dup_all = lax.all_gather(grad_up_pre, "data", axis=0)
        back_part = (jnp.einsum("atf,bef->atbe", dgate_all, gate_w, preferred_element_type=jnp.float32) + jnp.einsum("atf,bef->atbe", dup_all, up_w, preferred_element_type=jnp.float32)).astype(jnp.bfloat16)
        grad_in = (grad_loc.astype(jnp.float32) + to_rows(back_part).astype(jnp.float32)).astype(jnp.bfloat16)

        grad_down = lax.psum_scatter(jnp.einsum("atf,tbae->fbe", hid_all, grad_split, preferred_element_type=jnp.float32), "datb", scatter_dimension=1)
        grad_gate = lax.psum_scatter(jnp.einsum("tbae,atf->bef", tok_split, dgate_all, preferred_element_type=jnp.float32), "datb", scatter_dimension=0)
        grad_up = lax.psum_scatter(jnp.einsum("tbae,atf->bef", tok_split, dup_all, preferred_element_type=jnp.float32), "datb", scatter_dimension=0)
        return out, grad_in, grad_gate, grad_up, grad_down

    return jax.shard_map(local_step, mesh=mesh, in_specs=(ROW_SPEC, GATE_SPEC, GATE_SPEC, DOWN_SPEC, ROW_SPEC), out_specs=(ROW_SPEC, ROW_SPEC, GATE_SPEC, GATE_SPEC, DOWN_SPEC), check_vma=False)
```

profile of v0, /device:TPU:1, one launch (start us, length us, event | category | flops | bytes accessed | tf_op | source)
XLA Modules:
  0.0 1214.8 jit_solution(12560477444878683674)
XLA Ops:
  7.2 0.7 all-gather.12.cloned.1.call-update
  7.9 0.7 all-gather.24.cloned.1.call-update
  8.7 0.7 all-gather.22.cloned.1.call-update
  10.6 30.4 %all-gather.12.cloned.1.call-done = bf16[256,3584]{1,0:T(8,128)(2,1)} async-done(((bf16[64,3584]{1,0:T(8,128)(2,1)}), bf16[256,3584]{1,0:T(8,128)(2,1)}) %all-gather.12.cloned.1.call-update) | async-done | bytes 1835024 | tf_op jit(solution)/shard_map/all_gather | solution.py:30
  41.0 2.9 copy.35
  44.1 28.3 %all_to_all.28 = bf16[256,4,8,112]{0,3,1,2:T(8,128)(2,1)S(1)} all-to-all(bf16[256,4,8,112]{0,3,1,2:T(8,128)(2,1)S(1)} %copy.36), channel_id=1, replica_groups=mesh['datb'=4,'model'=4,'data'=8] {'data'}, dimensions={2} | all-to-all | bytes 3670016 | tf_op jit(solution)/shard_map/all_to_all | solution.py:31
  72.4 18.9 %all-gather.24.cloned.1.call-done = bf16[448,4736]{1,0:T(8,128)(2,1)} async-done(((bf16[112,4736]{1,0:T(8,128)(2,1)}), bf16[448,4736]{1,0:T(8,128)(2,1)}) %all-gather.24.cloned.1.call-update) | async-done | bytes 4243472 | tf_op jit(solution)/shard_map/all_gather | solution.py:27
  91.3 15.6 %bitcast_convert_fusion.1 = bf16[256,8,4736]{2,0,1:T(8,128)(2,1)} fusion(bf16[256,4,8,112]{0,3,1,2:T(8,128)(2,1)S(1)} %all_to_all.28, bf16[4,112,4736,1]{2,1,0,3:T(8,128)(2,1)} %bitcast.152), kind=kOutput, calls=%fused_computation.1 | convolution fusion | flops 8700297216 | bytes 25477120 | tf_op jit(solution)/shard_map/tbae,bef->taf/dot_general | solution.py:33
  107.0 35.0 %all-gather.22.cloned.1.call-done = bf16[448,4736]{1,0:T(8,128)(2,1)} async-done(((bf16[112,4736]{1,0:T(8,128)(2,1)}), bf16[448,4736]{1,0:T(8,128)(2,1)}) %all-gather.22.cloned.1.call-update) | async-done | bytes 4243472 | tf_op jit(solution)/shard_map/all_gather | solution.py:26
  142.0 15.7 %bitcast_convert_fusion.2 = bf16[256,8,4736]{2,0,1:T(8,128)(2,1)} fusion(bf16[256,4,8,112]{0,3,1,2:T(8,128)(2,1)S(1)} %all_to_all.28, bf16[4,112,4736,1]{2,1,0,3:T(8,128)(2,1)} %bitcast.154), kind=kOutput, calls=%fused_computation.2 | convolution fusion | flops 8700297216 | bytes 25477120 | tf_op jit(solution)/shard_map/tbae,bef->taf/dot_general | solution.py:32
  157.7 14.5 %all-gather.16.cloned.1.call-done = bf16[256,3584]{1,0:T(8,128)(2,1)} async-done(((bf16[64,3584]{1,0:T(8,128)(2,1)}), bf16[256,3584]{1,0:T(8,128)(2,1)}) %all-gather.16.cloned.1.call-update) | async-done | bytes 1835024 | tf_op jit(solution)/shard_map/all_gather | solution.py:43
  172.2 2.9 copy.39
  175.3 28.3 %all_to_all.29 = bf16[256,4,8,112]{0,3,1,2:T(8,128)(2,1)S(1)} all-to-all(bf16[256,4,8,112]{0,3,1,2:T(8,128)(2,1)S(1)} %copy.40), channel_id=1, replica_groups=mesh['datb'=4,'model'=4,'data'=8] {'data'}, dimensions={2} | all-to-all | bytes 3670016 | tf_op jit(solution)/shard_map/all_to_all | solution.py:44
  203.6 18.8 %all-gather.26.cloned.1.call-done = bf16[4736,448]{0,1:T(8,128)(2,1)} async-done(((bf16[4736,112]{0,1:T(8,128)(2,1)}), bf16[4736,448]{0,1:T(8,128)(2,1)}) %all-gather.26.cloned.1.call-update) | async-done | bytes 4243472 | tf_op jit(solution)/shard_map/all_gather | solution.py:28
  222.4 15.7 %bitcast_convert_fusion = bf16[256,8,4736]{2,0,1:T(8,128)(2,1)} fusion(bf16[256,4,8,112]{0,3,1,2:T(8,128)(2,1)S(1)} %all_to_all.29, bf16[4736,4,112,1]{0,2,1,3:T(8,128)(2,1)} %bitcast.156), kind=kOutput, calls=%fused_computation | convolution fusion | flops 8700297216 | bytes 25477120 | tf_op jit(solution)/shard_map/tbae,fbe->taf/dot_general | solution.py:45
  238.1 90.9 %reduce-scatter.15.cloned.1.call-done = bf16[256,1,4736]{2,0,1:T(8,128)(2,1)} async-done(((bf16[256,8,4736]{2,0,1:T(8,128)(2,1)}), bf16[256,1,4736]{2,0,1:T(8,128)(2,1)}) %reduce-scatter.15.cloned.1.call-update) | async-done | bytes 2424848 | tf_op jit(solution)/shard_map/reduce_scatter | solution.py:35
  329.0 106.4 %reduce-scatter.13.cloned.1.call-done = bf16[256,1,4736]{2,0,1:T(8,128)(2,1)} async-done(((bf16[256,8,4736]{2,0,1:T(8,128)(2,1)}), bf16[256,1,4736]{2,0,1:T(8,128)(2,1)}) %reduce-scatter.13.cloned.1.call-update) | async-done | bytes 2424848 | tf_op jit(solution)/shard_map/reduce_scatter | solution.py:34
  435.4 106.4 %reduce-scatter.17.cloned.1.call-done = bf16[256,1,4736]{2,0,1:T(8,128)(2,1)} async-done(((bf16[256,8,4736]{2,0,1:T(8,128)(2,1)}), bf16[256,1,4736]{2,0,1:T(8,128)(2,1)}) %reduce-scatter.17.cloned.1.call-update) | async-done | bytes 2424848 | tf_op jit(solution)/shard_map/reduce_scatter | solution.py:46
  541.7 6.8 fusion.24
  549.2 0.7 all-gather.14.cloned.1.call-update
  550.1 95.4 %all-gather.20.cloned.1.call-done = bf16[8,256,4736]{2,1,0:T(8,128)(2,1)} async-done(((bf16[1,256,4736]{2,1,0:T(8,128)(2,1)}), bf16[8,256,4736]{2,1,0:T(8,128)(2,1)}) %all-gather.20.cloned.1.call-update) | async-done | bytes 19398672 | tf_op jit(solution)/shard_map/all_gather | solution.py:50
  645.6 15.6 %fusion.2 = f32[8,256,4,112]{1,3,2,0:T(8,128)} fusion(bf16[4,112,4736,1]{2,1,0,3:T(8,128)(2,1)} %bitcast.153, bf16[8,256,4736]{2,1,0:T(8,128)(2,1)} %all-gather.20.cloned.1.call-done), kind=kOutput, calls=%fused_computation.5 | convolution fusion | flops 8690597888 | bytes 27312128 | tf_op jit(solution)/shard_map/atf,bef->atbe/dot_general | solution.py:51
  661.2 82.9 %all-gather.18.cloned.1.call-done = bf16[8,256,4736]{2,1,0:T(8,128)(2,1)} async-done(((bf16[1,256,4736]{2,1,0:T(8,128)(2,1)}), bf16[8,256,4736]{2,1,0:T(8,128)(2,1)}) %all-gather.18.cloned.1.call-update) | async-done | bytes 19398672 | tf_op jit(solution)/shard_map/all_gather | solution.py:49
  744.1 15.8 %add_convert_fusion = bf16[8,256,4,112]{1,3,2,0:T(8,128)(2,1)} fusion(f32[8,256,4,112]{1,3,2,0:T(8,128)} %fusion.2, bf16[4,112,4736,1]{2,1,0,3:T(8,128)(2,1)} %bitcast.155, bf16[8,256,4736]{2,1,0:T(8,128)(2,1)} %all-gather.18.cloned.1.call-done), kind=kOutput, calls=%fused_computation.33 | convolution fusion | flops 8692432896 | bytes 29147136 | tf_op jit(solution)/shard_map/atf,bef->atbe/dot_general | solution.py:51
  759.9 3.8 copy.41
  763.7 79.0 %all-gather.14.cloned.1.call-done = bf16[8,256,4736]{2,1,0:T(8,128)(2,1)} async-done(((bf16[1,256,4736]{2,1,0:T(8,128)(2,1)}), bf16[8,256,4736]{2,1,0:T(8,128)(2,1)}) %all-gather.14.cloned.1.call-update) | async-done | bytes 19398672 | tf_op jit(solution)/shard_map/all_gather | solution.py:39
  842.8 15.3 %fusion.32 = bf16[8,256,4,112]{1,3,2,0:T(8,128)(2,1)} fusion(bf16[4736,4,112,1]{0,2,1,3:T(8,128)(2,1)} %bitcast.157, bf16[8,256,4736]{2,1,0:T(8,128)(2,1)} %all-gather.14.cloned.1.call-done), kind=kOutput, calls=%fused_computation.34 | convolution fusion | flops 8691515392 | bytes 25477120 | tf_op jit(solution)/shard_map/atf,fbe->atbe/dot_general | solution.py:40
  858.0 3.9 copy.37
  862.2 15.7 %fusion.12 = f32[4736,4,112]{0,2,1:T(8,128)} fusion(bf16[256,4,8,112]{0,3,1,2:T(8,128)(2,1)S(1)} %all_to_all.29, bf16[8,256,4736]{2,1,0:T(8,128)(2,1)} %all-gather.14.cloned.1.call-done), kind=kOutput, calls=%fused_computation.15 | convolution fusion | flops 8690597888 | bytes 29720576 | tf_op jit(solution)/shard_map/atf,tbae->fbe/dot_general | solution.py:54
  877.9 1.4 copy-done.2
  879.4 15.7 %fusion.15 = f32[4,112,4736]{2,1,0:T(8,128)} fusion(bf16[256,4,8,112]{0,3,1,2:T(8,128)(2,1)S(1)} %copy-done.2, bf16[8,256,4736]{2,1,0:T(8,128)(2,1)} %all-gather.18.cloned.1.call-done), kind=kOutput, calls=%fused_computation.16 | convolution fusion | flops 8690597888 | bytes 29720576 | tf_op jit(solution)/shard_map/tbae,atf->bef/dot_general | solution.py:55
  895.4 15.7 %fusion.18 = f32[4,112,4736]{2,1,0:T(8,128)} fusion(bf16[256,4,8,112]{0,3,1,2:T(8,128)(2,1)S(1)} %copy-done.2, bf16[8,256,4736]{2,1,0:T(8,128)(2,1)} %all-gather.20.cloned.1.call-done), kind=kOutput, calls=%fused_computation.17 | convolution fusion | flops 8690597888 | bytes 29720576 | tf_op jit(solution)/shard_map/tbae,atf->bef/dot_general | solution.py:56
  911.2 0.6 copy-done.3
  912.4 42.3 %all-reduce.5.cloned.1.call-done = (bf16[8,4,64,4,112]{4,2,1,3,0:T(8,128)(2,1)}, bf16[8,4,64,4,112]{4,2,1,3,0:T(8,128)(2,1)}) async-done(((bf16[8,4,64,4,112]{4,2,1,3,0:T(8,128)(2,1)}, bf16[8,4,64,4,112]{4,2,1,3,0:T(8,128)(2,1)}), (bf16[8,4,64,4,112]{4,2,1,3,0:T(8,128)(2,1)}, bf16[8,4,64,4,112]{4,2,1,3,0:T(8,128)(2,1)})) %all-reduce.5.cloned.1.call-update) | async-done | bytes 3670032
  954.7 2.5 dynamic-slice_bitcast_fusion.1
  957.2 5.2 all-to-all-start.1
  962.4 2.6 dynamic-slice_bitcast_fusion
  965.0 6.6 all-to-all-done.1
  971.6 4.6 all-to-all-start.3
  976.3 0.6 copy.38
  976.9 0.6 reshape.140
  977.5 7.8 all-to-all-done.3
  985.4 0.6 copy.42
  986.1 0.6 reshape.142
  986.7 2.1 add_convert_fusion.1
  988.8 50.6 %reduce-scatter.23.cloned.1.call-done = f32[4736,1,112]{0,2,1:T(8,128)} async-done(((f32[4736,4,112]{0,2,1:T(8,128)}), f32[4736,1,112]{0,2,1:T(8,128)}) %reduce-scatter.23.cloned.1.call-update) | async-done | bytes 2121744 | tf_op jit(solution)/shard_map/reduce_scatter | solution.py:54
  1039.4 84.2 %reduce-scatter.19.cloned.1.call-done = f32[1,112,4736]{2,1,0:T(8,128)} async-done(((f32[4,112,4736]{2,1,0:T(8,128)}), f32[1,112,4736]{2,1,0:T(8,128)}) %reduce-scatter.19.cloned.1.call-update) | async-done | bytes 2121744 | tf_op jit(solution)/shard_map/reduce_scatter | solution.py:55
  1123.6 84.2 %reduce-scatter.21.cloned.1.call-done = f32[1,112,4736]{2,1,0:T(8,128)} async-done(((f32[4,112,4736]{2,1,0:T(8,128)}), f32[1,112,4736]{2,1,0:T(8,128)}) %reduce-scatter.21.cloned.1.call-update) | async-done | bytes 2121744 | tf_op jit(solution)/shard_map/reduce_scatter | solution.py:56
  (37 shorter events, 4.1 us)
Async XLA Ops:
  7.2 33.9 %all-gather.12.cloned.1.call-start = ((), (), s32[]{:S(2)}) async-start(), calls=%async_computation.10 | async-start | bytes 2293760 | tf_op jit(solution)/shard_map/all_gather | solution.py:30
  7.9 83.4 %all-gather.24.cloned.1.call-start = ((), (), s32[]{:S(2)}) async-start(), calls=%async_computation.22 | async-start | bytes 5304320 | tf_op jit(solution)/shard_map/all_gather | solution.py:27
  8.6 133.3 %all-gather.22.cloned.1.call-start = ((), (), s32[]{:S(2)}) async-start(), calls=%async_computation.21 | async-start | bytes 5304320 | tf_op jit(solution)/shard_map/all_gather | solution.py:26
  9.4 162.8 %all-gather.16.cloned.1.call-start = ((), (), s32[]{:S(2)}) async-start(), calls=%async_computation.14 | async-start | bytes 2293760 | tf_op jit(solution)/shard_map/all_gather | solution.py:43
  10.0 212.4 %all-gather.26.cloned.1.call-start = ((), (), s32[]{:S(2)}) async-start(), calls=%async_computation.23 | async-start | bytes 5304320 | tf_op jit(solution)/shard_map/all_gather | solution.py:28
  10.5 318.4 %reduce-scatter.15.cloned.1.call-start = ((), (), s32[]{:S(2)}) async-start(), calls=%async_computation.12 | async-start | bytes 21823488 | tf_op jit(solution)/shard_map/reduce_scatter | solution.py:35
  72.4 69.6 %copy-start.1 = (bf16[256,4,8,112]{0,3,1,2:T(8,128)(2,1)}, bf16[256,4,8,112]{0,3,1,2:T(8,128)(2,1)S(1)}, u32[]{:S(2)}) copy-start(bf16[256,4,8,112]{0,3,1,2:T(8,128)(2,1)S(1)} %all_to_all.28) | copy-start | bytes 5505028
  106.9 328.4 %reduce-scatter.13.cloned.1.call-start = ((), (), s32[]{:S(2)}) async-start(), calls=%async_computation.11 | async-start | bytes 21823488 | tf_op jit(solution)/shard_map/reduce_scatter | solution.py:34
  157.7 384.1 %reduce-scatter.17.cloned.1.call-start = ((), (), s32[]{:S(2)}) async-start(), calls=%async_computation.15 | async-start | bytes 21823488 | tf_op jit(solution)/shard_map/reduce_scatter | solution.py:46
  238.1 407.5 %all-gather.20.cloned.1.call-start = ((), (), s32[]{:S(2)}) async-start(), calls=%async_computation.17 | async-start | bytes 21823488 | tf_op jit(solution)/shard_map/all_gather | solution.py:50
  548.6 195.5 %all-gather.18.cloned.1.call-start = ((), (), s32[]{:S(2)}) async-start(), calls=%async_computation.16 | async-start | bytes 21823488 | tf_op jit(solution)/shard_map/all_gather | solution.py:49
  549.2 293.6 %all-gather.14.cloned.1.call-start = ((), (), s32[]{:S(2)}) async-start(), calls=%async_computation.13 | async-start | bytes 21823488 | tf_op jit(solution)/shard_map/all_gather | solution.py:39
  549.9 404.8 %all-reduce.5.cloned.1.call-start = ((), (), s32[]{:S(2)}) async-start(), calls=%async_computation.24 | async-start | bytes 8388608
  861.9 177.4 %reduce-scatter.23.cloned.1.call-start = ((), (), s32[]{:S(2)}) async-start(), calls=%async_computation.20 | async-start | bytes 10608640 | tf_op jit(solution)/shard_map/reduce_scatter | solution.py:54
  877.9 1.5 copy-start.2
  877.9 245.7 %reduce-scatter.19.cloned.1.call-start = ((), (), s32[]{:S(2)}) async-start(), calls=%async_computation.18 | async-start | bytes 10608640 | tf_op jit(solution)/shard_map/reduce_scatter | solution.py:55
  895.1 312.7 %reduce-scatter.21.cloned.1.call-start = ((), (), s32[]{:S(2)}) async-start(), calls=%async_computation.19 | async-start | bytes 10608640 | tf_op jit(solution)/shard_map/reduce_scatter | solution.py:56
  911.2 0.7 copy-start.3
  957.2 14.3 %all-to-all-start.1 = ((bf16[8,64,4,1,112]{4,1,3,2,0:T(8,128)(2,1)}), bf16[8,64,4,1,112]{4,1,3,2,0:T(8,128)(2,1)S(1)}, u32[]{:S(2)}, u32[]{:S(2)}) async-start(bf16[8,64,4,1,112]{4,1,3,2,0:T(8,128)(2,1)} %dynamic-slice_bitcast_fusion.1), calls=%async_computation.3 | async-start | bytes 1048576 | tf_op jit(solution)/shard_map/all_to_all | solution.py:23
  971.6 13.8 %all-to-all-start.3 = ((bf16[8,64,4,1,112]{4,1,3,2,0:T(8,128)(2,1)}), bf16[8,64,4,1,112]{4,1,3,2,0:T(8,128)(2,1)S(1)}, u32[]{:S(2)}, u32[]{:S(2)}) async-start(bf16[8,64,4,1,112]{4,1,3,2,0:T(8,128)(2,1)} %dynamic-slice_bitcast_fusion), calls=%async_computation.6 | async-start | bytes 1048576 | tf_op jit(solution)/shard_map/all_to_all | solution.py:23
  976.9 9.8 copy-start
Sparse Core Ops, SparseCore 0:
  9.6 31.3 all-gather.11
  42.7 48.6 all-gather.23
  93.0 48.9 all-gather.21
  143.5 28.6 all-gather.15
  173.7 48.6 all-gather.25
  224.7 104.2 reduce-scatter.14
  331.5 103.8 reduce-scatter.12
  437.8 103.8 reduce-scatter.16
  548.7 96.8 all-gather.19
  647.1 96.9 all-gather.17
  745.8 96.9 all-gather.13
  862.0 92.6 all-reduce.4
  957.8 81.5 reduce-scatter.22
  1042.3 81.2 reduce-scatter.18
  1126.5 81.2 reduce-scatter.20
where the time goes:
time: 1220 us; the launch traced here: 1210 us
  waiting for transfers between devices  959 us (79%)
  matrix products  141 us (12%)
  blocking collectives  56.7 us (5%)
  local copies, waits for them, and re-layouts  24 us (2%)
  between operations  14.5 us (1%)
    reduce_scatter x1, waiting for transfers between devices, local_step(): lax.psum_scatter(grad_hid_part, 'data', scatter_dimension=1)  106 us
    reduce_scatter x1, waiting for transfers between devices, local_step(): lax.psum_scatter(gate_part, 'data', scatter_dimension=1).astype(jnp.float32)  106 us
    all_gather x1, waiting for transfers between devices, local_step(): dup_all = lax.all_gather(grad_up_pre, 'data', axis=0)  95.4 us
    reduce_scatter x1, waiting for transfers between devices, local_step(): lax.psum_scatter(up_part, 'data', scatter_dimension=1).astype(jnp.float32)  90.9 us
    reduce_scatter x1, waiting for transfers between devices, local_step(): lax.psum_scatter(jnp.einsum('tbae,atf->bef', tok_split, dgate_all, prefer...  84.2 us
    reduce_scatter x1, waiting for transfers between devices, local_step(): lax.psum_scatter(jnp.einsum('tbae,atf->bef', tok_split, dup_all, preferre...  84.2 us
    all_gather x1, waiting for transfers between devices, local_step(): dgate_all = lax.all_gather(grad_gate_pre, 'data', axis=0)  82.9 us
    all_gather x1, waiting for transfers between devices, local_step(): hid_all = lax.all_gather(hidden, 'data', axis=0)  79 us
  transfers between devices with their start and end apart: 17, of which 17 were waited for; matrix products, arithmetic and copies ran while one was open for 12% of the time, Pallas kernels for 0%

commit v1 on v0

v1 whole, which is shorter than its diff:
```python
import jax
import jax.numpy as jnp
from jax import lax
from jax.sharding import PartitionSpec as P

ROW_SPEC = P(("datb", "data", "model"), None)
GATE_SPEC = P(("datb", "data"), "model")
DOWN_SPEC = P("model", ("datb", "data"))


def solution(mesh):
    data_size = mesh.shape["data"]

    def local_step(tok_loc, wg_loc, wu_loc, wd_loc, grad_loc):
        def gate_like(w):
            w = lax.all_to_all(w, "data", 1, 0, tiled=True)
            return lax.all_gather(w, "datb", axis=0, tiled=True)

        wg = gate_like(wg_loc)
        wu = gate_like(wu_loc)
        wd = lax.all_gather(lax.all_to_all(wd_loc, "data", 0, 1, tiled=True), "datb", axis=1, tiled=True)

        tok = lax.all_gather(tok_loc, ("data", "model"), axis=0, tiled=True)
        grad = lax.all_gather(grad_loc, ("data", "model"), axis=0, tiled=True)

        gate_pre = jnp.dot(tok, wg, preferred_element_type=jnp.float32).astype(jnp.bfloat16).astype(jnp.float32)
        up_pre = jnp.dot(tok, wu, preferred_element_type=jnp.float32).astype(jnp.bfloat16).astype(jnp.float32)
        grad_hid = jnp.dot(grad, wd.T, preferred_element_type=jnp.float32).astype(jnp.bfloat16).astype(jnp.float32)
        sig = jax.nn.sigmoid(gate_pre)
        silu = gate_pre * sig
        hidden = (silu * up_pre).astype(jnp.bfloat16)
        dgate = (grad_hid * up_pre * sig * (1.0 + gate_pre * (1.0 - sig))).astype(jnp.bfloat16)
        dup = (grad_hid * silu).astype(jnp.bfloat16)

        g_gate = jnp.dot(tok.T, dgate, preferred_element_type=jnp.float32)
        g_up = jnp.dot(tok.T, dup, preferred_element_type=jnp.float32)
        g_down = jnp.dot(hidden.T, grad, preferred_element_type=jnp.float32)

        down_part = jnp.dot(hidden, wd, preferred_element_type=jnp.float32).astype(jnp.bfloat16)
        back_part = (jnp.dot(dgate, wg.T, preferred_element_type=jnp.float32) + jnp.dot(dup, wu.T, preferred_element_type=jnp.float32)).astype(jnp.bfloat16)

        def to_rows(part):
            return lax.psum_scatter(part, ("data", "model"), scatter_dimension=0, tiled=True)

        out = (tok_loc.astype(jnp.float32) + to_rows(down_part).astype(jnp.float32)).astype(jnp.bfloat16)
        grad_in = (grad_loc.astype(jnp.float32) + to_rows(back_part).astype(jnp.float32)).astype(jnp.bfloat16)

        def grad_gate_like(g):
            g = lax.psum_scatter(g, "datb", scatter_dimension=0, tiled=True)
            return lax.all_to_all(g, "data", 0, 1, tiled=True)

        grad_gate = grad_gate_like(g_gate)
        grad_up = grad_gate_like(g_up)
        grad_down = lax.all_to_all(lax.psum_scatter(g_down, "datb", scatter_dimension=1, tiled=True), "data", 1, 0, tiled=True)
        return out, grad_in, grad_gate, grad_up, grad_down

    return jax.shard_map(local_step, mesh=mesh, in_specs=(ROW_SPEC, GATE_SPEC, GATE_SPEC, DOWN_SPEC, ROW_SPEC), out_specs=(ROW_SPEC, ROW_SPEC, GATE_SPEC, GATE_SPEC, DOWN_SPEC), check_vma=False)
```

time: 1220 us -> 819 us (0.67)
  waiting for transfers between devices: 959 us -> 531 us
  matrix products: 141 us -> 158 us
    reduce_scatter x6 -> x5, waiting for transfers between devices: 523 us -> 304 us  [the longest x2 181 us: to_rows(): lax.psum_scatter(part, ('data', 'model'), scatter_dimension=0, tiled=True)]
    all_gather x8 -> x5, waiting for transfers between devices: 375 us -> 207 us  [the longest x1 70.6 us: local_step(): tok = lax.all_gather(tok_loc, ('data', 'model'), axis=0, tiled=True)]
    unnamed x16 -> x10, waiting for transfers between devices: 46.8 us -> 1.35 us
    all_to_all x0 -> x12, local copies, waits for them, and re-layouts: none -> 19.4 us  [the longest x4 8.25 us: grad_gate_like(): return lax.all_to_all(g, 'data', 0, 1, tiled=True)]
    dot_general x9, matrix products: 141 us -> 158 us  [the longest x1 21.9 us: local_step(): jnp.dot(dgate, wg.T, preferred_element_type=jnp.float32)]
    all_to_all x2 -> x3, blocking collectives: 56.7 us -> 61.8 us  [the longest x2 41.8 us: gate_like(): w = lax.all_to_all(w, 'data', 1, 0, tiled=True)]
  transfers between devices with their start and end apart: 17 -> 13, of which waited for: 17 -> 10; matrix products, arithmetic and copies ran while one was open for 12% -> 22% of each run, Pallas kernels for 0% -> 0%
where the time goes in v1:
time: 819 us; the launch traced here: 814 us
  waiting for transfers between devices  531 us (65%)
  matrix products  158 us (19%)
  blocking collectives  61.8 us (8%)
  local copies, waits for them, and re-layouts  28.7 us (4%)
  starting transfers between devices  16.7 us (2%)
  between operations  14.5 us (2%)
    reduce_scatter x2, waiting for transfers between devices, to_rows(): lax.psum_scatter(part, ('data', 'model'), scatter_dimension=0, tiled=True)  181 us
    reduce_scatter x2, waiting for transfers between devices, grad_gate_like(): g = lax.psum_scatter(g, 'datb', scatter_dimension=0, tiled=True)  122 us
    all_gather x1, waiting for transfers between devices, local_step(): tok = lax.all_gather(tok_loc, ('data', 'model'), axis=0, tiled=True)  70.6 us
    all_gather x1, waiting for transfers between devices, local_step(): grad = lax.all_gather(grad_loc, ('data', 'model'), axis=0, tiled=True)  55.8 us
    all_gather x2, waiting for transfers between devices, gate_like(): return lax.all_gather(w, 'datb', axis=0, tiled=True)  45.2 us
    all_to_all x2, blocking collectives, gate_like(): w = lax.all_to_all(w, 'data', 1, 0, tiled=True)  41.8 us
    all_gather x1, waiting for transfers between devices, local_step(): lax.all_gather(lax.all_to_all(wd_loc, 'data', 0, 1, tiled=True), 'datb',...  35.1 us
    dot_general x1, matrix products, local_step(): jnp.dot(dgate, wg.T, preferred_element_type=jnp.float32)  21.9 us
  transfers between devices with their start and end apart: 13, of which 10 were waited for; matrix products, arithmetic and copies ran while one was open for 22% of the time, Pallas kernels for 0%

profile of v1, /device:TPU:1, one launch (start us, length us, event | category | flops | bytes accessed | tf_op | source)
XLA Modules:
  0.0 814.2 jit_solution(5467461556183472278)
XLA Ops:
  7.2 2.6 all_to_all.84
  9.8 0.1 copy.19
  10.0 21.8 %all_to_all.114 = bf16[112,8,592]{2,0,1:T(8,128)(2,1)} all-to-all(bf16[112,8,592]{2,0,1:T(8,128)(2,1)S(1)} %copy.19), channel_id=1, replica_groups=mesh['datb'=4,'model'=4,'data'=8] {'data'}, dimensions={1} | all-to-all | bytes 2121728 | tf_op jit(solution)/shard_map/all_to_all | solution.py:16
  31.8 0.7 all-gather.6.cloned.1.call-update
  32.6 1.5 all_to_all.88
  34.1 0.1 copy.20
  34.3 20.0 %all_to_all.115 = bf16[112,8,592]{2,0,1:T(8,128)(2,1)} all-to-all(bf16[112,8,592]{2,0,1:T(8,128)(2,1)S(1)} %copy.20), channel_id=1, replica_groups=mesh['datb'=4,'model'=4,'data'=8] {'data'}, dimensions={1} | all-to-all | bytes 2121728 | tf_op jit(solution)/shard_map/all_to_all | solution.py:16
  54.3 0.5 all-gather.14.cloned.1.call-update
  54.9 1.5 all_to_all.92
  56.5 0.1 copy.21
  56.6 20.0 %all_to_all.116 = bf16[8,592,112]{1,2,0:T(8,128)(2,1)} all-to-all(bf16[8,592,112]{1,2,0:T(8,128)(2,1)S(1)} %copy.21), channel_id=1, replica_groups=mesh['datb'=4,'model'=4,'data'=8] {'data'}, dimensions={0} | all-to-all | bytes 2121728 | tf_op jit(solution)/shard_map/all_to_all | solution.py:21
  76.6 0.6 reduce-scatter.14.cloned.1.call-start
  77.2 6.7 all-gather.8.cloned.1.call-done
  83.9 70.6 %all-gather.6.cloned.1.call-done = bf16[2048,3584]{1,0:T(8,128)(2,1)} async-done(((bf16[64,3584]{1,0:T(8,128)(2,1)}), bf16[2048,3584]{1,0:T(8,128)(2,1)}) %all-gather.6.cloned.1.call-update) | async-done | bytes 14680080 | tf_op jit(solution)/shard_map/all_gather | solution.py:23
  154.5 13.6 %convolution_convert_fusion.3 = bf16[2048,592]{0,1:T(8,128)(2,1)S(1)} fusion(bf16[2048,3584]{1,0:T(8,128)(2,1)} %all-gather.6.cloned.1.call-done, bf16[3584,592]{1,0:T(8,128)(2,1)} %all-gather.8.cloned.1.call-done), kind=kOutput, calls=%fused_computation.21 | convolution fusion | flops 8691810304 | bytes 21348352 | tf_op jit(solution)/shard_map/dot_general | solution.py:26
  168.2 38.5 %all-gather.10.cloned.1.call-done = bf16[3584,592]{1,0:T(8,128)(2,1)} async-done(((bf16[896,592]{1,0:T(8,128)(2,1)}), bf16[3584,592]{1,0:T(8,128)(2,1)}) %all-gather.10.cloned.1.call-update) | async-done | bytes 4243472 | tf_op jit(solution)/shard_map/all_gather | solution.py:17
  206.7 14.7 %convolution_convert_fusion.2 = bf16[2048,592]{0,1:T(8,128)(2,1)} fusion(bf16[2048,3584]{1,0:T(8,128)(2,1)} %all-gather.6.cloned.1.call-done, bf16[3584,592]{1,0:T(8,128)(2,1)} %all-gather.10.cloned.1.call-done), kind=kOutput, calls=%fused_computation.20 | convolution fusion | flops 8691810304 | bytes 21348352 | tf_op jit(solution)/shard_map/dot_general | solution.py:27
  221.4 55.8 %all-gather.14.cloned.1.call-done = bf16[2048,3584]{1,0:T(8,128)(2,1)} async-done(((bf16[64,3584]{1,0:T(8,128)(2,1)}), bf16[2048,3584]{1,0:T(8,128)(2,1)}) %all-gather.14.cloned.1.call-update) | async-done | bytes 14680080 | tf_op jit(solution)/shard_map/all_gather | solution.py:24
  277.2 16.8 %fusion.11 = f32[592,3584]{1,0:T(8,128)} fusion(bf16[2048,3584]{1,0:T(8,128)(2,1)} %all-gather.14.cloned.1.call-done, bf16[2048,592]{0,1:T(8,128)(2,1)} %convolution_convert_fusion.2, bf16[2048,592]{0,1:T(8,128)(2,1)S(1)} %convolution_convert_fusion.3), kind=kOutput, calls=%fused_computation.24 | convolution fusion | flops 8700297216 | bytes 28016640 | tf_op jit(solution)/shard_map/dot_general | solution.py:37
  294.0 0.0 reduce-scatter.10.cloned.1.call-start
  294.1 35.1 %all-gather.12.cloned.1.call-done = bf16[592,3584]{0,1:T(8,128)(2,1)} async-done(((bf16[592,896]{0,1:T(8,128)(2,1)}), bf16[592,3584]{0,1:T(8,128)(2,1)}) %all-gather.12.cloned.1.call-update) | async-done | bytes 4243472 | tf_op jit(solution)/shard_map/all_gather | solution.py:21
  329.2 14.8 %convolution_convert_fusion.1 = bf16[2048,592]{0,1:T(8,128)(2,1)} fusion(bf16[2048,3584]{1,0:T(8,128)(2,1)} %all-gather.14.cloned.1.call-done, bf16[592,3584]{0,1:T(8,128)(2,1)} %all-gather.12.cloned.1.call-done), kind=kOutput, calls=%fused_computation.19 | convolution fusion | flops 8691810304 | bytes 21348352 | tf_op jit(solution)/shard_map/dot_general | solution.py:28
  344.0 18.2 %convolution_bitcast_fusion.1 = f32[3584,592]{0,1:T(8,128)} fusion(bf16[2048,3584]{1,0:T(8,128)(2,1)} %all-gather.6.cloned.1.call-done, bf16[2048,592]{0,1:T(8,128)(2,1)S(1)} %copy-done.4, bf16[2048,592]{0,1:T(8,128)(2,1)} %convolution_convert_fusion.1, bf16[2048,592]{0,1:T(8,128)(2,1)S(1)} %convolution_convert_fusion.3), kind=kOutput, calls=%fused_computation.6 | convolution fusion | flops 8706359296 | bytes 30441472 | tf_op jit(solution)/shard_map/dot_general | solution.py:35
  362.3 0.0 reduce-scatter.12.cloned.1.call-start
  362.3 16.9 %convolution_bitcast_fusion = f32[3584,592]{0,1:T(8,128)} fusion(bf16[2048,3584]{1,0:T(8,128)(2,1)} %all-gather.6.cloned.1.call-done, bf16[2048,592]{0,1:T(8,128)(2,1)} %convolution_convert_fusion.1, bf16[2048,592]{0,1:T(8,128)(2,1)S(1)} %convolution_convert_fusion.3), kind=kOutput, calls=%fused_computation.5 | convolution fusion | flops 8700297216 | bytes 28016640 | tf_op jit(solution)/shard_map/dot_general | solution.py:36
  379.2 0.0 reduce-scatter.6.cloned.1.call-start
  379.3 19.3 %convolution_convert_fusion = bf16[2048,3584]{1,0:T(8,128)(2,1)} fusion(bf16[592,3584]{0,1:T(8,128)(2,1)} %all-gather.12.cloned.1.call-done, bf16[2048,592]{0,1:T(8,128)(2,1)} %convolution_convert_fusion.2, bf16[2048,592]{0,1:T(8,128)(2,1)S(1)} %convolution_convert_fusion.3), kind=kOutput, calls=%fused_computation.1 | convolution fusion | flops 8707637248 | bytes 23773184 | tf_op jit(solution)/shard_map/dot_general | solution.py:39
  398.6 21.9 %fusion.15 = f32[2048,3584]{1,0:T(8,128)} fusion(bf16[3584,592]{1,0:T(8,128)(2,1)} %all-gather.8.cloned.1.call-done, bf16[2048,592]{0,1:T(8,128)(2,1)} %convolution_convert_fusion.2, bf16[2048,592]{0,1:T(8,128)(2,1)} %convolution_convert_fusion.1, bf16[2048,592]{0,1:T(8,128)(2,1)S(1)} %convolution_convert_fusion.3), kind=kOutput, calls=%fused_computation.25 | convolution fusion | flops 8706359296 | bytes 40878080 | tf_op jit(solution)/shard_map/dot_general | solution.py:40
  420.6 21.6 %add_convert_fusion = bf16[2048,3584]{1,0:T(8,128)(2,1)} fusion(f32[2048,3584]{1,0:T(8,128)} %fusion.15, bf16[3584,592]{1,0:T(8,128)(2,1)} %all-gather.10.cloned.1.call-done, bf16[2048,592]{0,1:T(8,128)(2,1)} %convolution_convert_fusion.1, bf16[2048,592]{0,1:T(8,128)(2,1)S(1)} %convolution_convert_fusion.3), kind=kOutput, calls=%fused_computation | convolution fusion | flops 8714977280 | bytes 53133312 | tf_op jit(solution)/shard_map/dot_general | solution.py:40
  442.2 3.1 copy.26
  445.3 5.2 all-to-all-start.5
  450.5 46.9 %reduce-scatter.10.cloned.1.call-done = f32[896,592]{0,1:T(8,128)} async-done(((f32[3584,592]{0,1:T(8,128)}), f32[896,592]{0,1:T(8,128)}) %reduce-scatter.10.cloned.1.call-update) | async-done | bytes 2121744 | tf_op jit(solution)/shard_map/reduce_scatter | solution.py:49
  497.4 3.1 copy.22
  500.5 5.2 all-to-all-start.3
  505.6 75.5 %reduce-scatter.12.cloned.1.call-done = f32[896,592]{0,1:T(8,128)} async-done(((f32[3584,592]{0,1:T(8,128)}), f32[896,592]{0,1:T(8,128)}) %reduce-scatter.12.cloned.1.call-update) | async-done | bytes 2121744 | tf_op jit(solution)/shard_map/reduce_scatter | solution.py:49
  581.2 3.1 copy.24
  584.3 5.4 all-to-all-start.4
  589.7 2.2 copy.27
  591.9 3.0 all_to_all.107
  594.8 2.4 copy.23
  597.2 1.7 all_to_all.99
  598.9 18.9 %all-to-all-done.4 = f32[8,112,592]{2,1,0:T(8,128)} async-done(((f32[8,112,592]{2,1,0:T(8,128)}), f32[8,112,592]{2,1,0:T(8,128)}, u32[]{:S(2)}, u32[]{:S(2)}) %all-to-all-start.4) | async-done | bytes 2121760 | tf_op jit(solution)/shard_map/all_to_all | solution.py:50
  617.9 2.4 copy.25
  620.3 1.7 all_to_all.103
  622.0 70.5 %reduce-scatter.6.cloned.1.call-done = bf16[64,3584]{1,0:T(8,128)(2,1)} async-done(((bf16[2048,3584]{1,0:T(8,128)(2,1)}), bf16[64,3584]{1,0:T(8,128)(2,1)}) %reduce-scatter.6.cloned.1.call-update) | async-done | bytes 458768 | tf_op jit(solution)/shard_map/reduce_scatter | solution.py:43
  692.6 1.9 add_convert_fusion.2
  694.4 110.9 %reduce-scatter.8.cloned.1.call-done = bf16[64,3584]{1,0:T(8,128)(2,1)} async-done(((bf16[2048,3584]{1,0:T(8,128)(2,1)}), bf16[64,3584]{1,0:T(8,128)(2,1)}) %reduce-scatter.8.cloned.1.call-update) | async-done | bytes 458768 | tf_op jit(solution)/shard_map/reduce_scatter | solution.py:43
  805.3 1.9 add_convert_fusion.1
  (27 shorter events, 0.4 us)
Async XLA Ops:
  7.2 25.4 %copy-start.2 = (bf16[112,4736]{1,0:T(8,128)(2,1)S(1)}, bf16[112,4736]{1,0:T(8,128)(2,1)}, u32[]{:S(2)}) copy-start(bf16[112,4736]{1,0:T(8,128)(2,1)} %param.7) | copy-start | bytes 3182596
  7.2 76.7 %all-gather.8.cloned.1.call-start = ((), (), s32[]{:S(2)}) async-start(), calls=%async_computation.12 | async-start | bytes 5734400 | tf_op jit(solution)/shard_map/all_gather | solution.py:17
  31.8 23.2 %copy-start.3 = (bf16[4736,112]{0,1:T(8,128)(2,1)S(1)}, bf16[4736,112]{0,1:T(8,128)(2,1)}, u32[]{:S(2)}) copy-start(bf16[4736,112]{0,1:T(8,128)(2,1)} %param.8) | copy-start | bytes 3182596
  31.8 122.8 %all-gather.6.cloned.1.call-start = ((), (), s32[]{:S(2)}) async-start(), calls=%async_computation.11 | async-start | bytes 15138816 | tf_op jit(solution)/shard_map/all_gather | solution.py:23
  32.5 174.2 %all-gather.10.cloned.1.call-start = ((), (), s32[]{:S(2)}) async-start(), calls=%async_computation.13 | async-start | bytes 5734400 | tf_op jit(solution)/shard_map/all_gather | solution.py:17
  54.3 222.9 %all-gather.14.cloned.1.call-start = ((), (), s32[]{:S(2)}) async-start(), calls=%async_computation.16 | async-start | bytes 15138816 | tf_op jit(solution)/shard_map/all_gather | solution.py:24
  54.9 274.3 %all-gather.12.cloned.1.call-start = ((), (), s32[]{:S(2)}) async-start(), calls=%async_computation.14 | async-start | bytes 5734400 | tf_op jit(solution)/shard_map/all_gather | solution.py:21
  76.6 365.6 %reduce-scatter.14.cloned.1.call-start = ((), (), s32[]{:S(2)}) async-start(), calls=%async_computation.20 | async-start | bytes 10608640 | tf_op jit(solution)/shard_map/reduce_scatter | solution.py:54
  294.0 203.3 %reduce-scatter.10.cloned.1.call-start = ((), (), s32[]{:S(2)}) async-start(), calls=%async_computation.18 | async-start | bytes 10608640 | tf_op jit(solution)/shard_map/reduce_scatter | solution.py:49
  329.2 14.8 %copy-start.4 = (bf16[2048,592]{0,1:T(8,128)(2,1)S(1)}, bf16[2048,592]{0,1:T(8,128)(2,1)}, u32[]{:S(2)}) copy-start(bf16[2048,592]{0,1:T(8,128)(2,1)} %convolution_convert_fusion.2) | copy-start | bytes 7274500
  362.3 218.9 %reduce-scatter.12.cloned.1.call-start = ((), (), s32[]{:S(2)}) async-start(), calls=%async_computation.19 | async-start | bytes 10608640 | tf_op jit(solution)/shard_map/reduce_scatter | solution.py:49
  379.2 313.3 %reduce-scatter.6.cloned.1.call-start = ((), (), s32[]{:S(2)}) async-start(), calls=%async_computation.15 | async-start | bytes 15138816 | tf_op jit(solution)/shard_map/reduce_scatter | solution.py:43
  398.6 406.7 %reduce-scatter.8.cloned.1.call-start = ((), (), s32[]{:S(2)}) async-start(), calls=%async_computation.17 | async-start | bytes 15138816 | tf_op jit(solution)/shard_map/reduce_scatter | solution.py:43
  445.3 55.1 %all-to-all-start.5 = ((f32[592,8,112]{0,2,1:T(8,128)}), f32[592,8,112]{0,2,1:T(8,128)S(1)}, u32[]{:S(2)}, u32[]{:S(2)}) async-start(f32[592,8,112]{0,2,1:T(8,128)} %bitcast.38), calls=%async_computation.10 | async-start | bytes 4587520 | tf_op jit(solution)/shard_map/all_to_all | solution.py:54
  500.5 83.8 %all-to-all-start.3 = ((f32[8,112,592]{2,1,0:T(8,128)}), f32[8,112,592]{2,1,0:T(8,128)}, u32[]{:S(2)}, u32[]{:S(2)}) async-start(f32[8,112,592]{2,1,0:T(8,128)} %bitcast.37), calls=%async_computation.6 | async-start | bytes 4587520 | tf_op jit(solution)/shard_map/all_to_all | solution.py:50
  584.3 33.6 %all-to-all-start.4 = ((f32[8,112,592]{2,1,0:T(8,128)}), f32[8,112,592]{2,1,0:T(8,128)}, u32[]{:S(2)}, u32[]{:S(2)}) async-start(f32[8,112,592]{2,1,0:T(8,128)} %bitcast.36), calls=%async_computation.8 | async-start | bytes 4587520 | tf_op jit(solution)/shard_map/all_to_all | solution.py:50
  598.9 93.6 %copy-start = (bf16[64,3584]{1,0:T(8,128)(2,1)S(1)}, bf16[64,3584]{1,0:T(8,128)(2,1)}, u32[]{:S(2)}) copy-start(bf16[64,3584]{1,0:T(8,128)(2,1)} %param.5) | copy-start | bytes 1376260
  617.9 187.4 %copy-start.1 = (bf16[64,3584]{1,0:T(8,128)(2,1)S(1)}, bf16[64,3584]{1,0:T(8,128)(2,1)}, u32[]{:S(2)}) copy-start(bf16[64,3584]{1,0:T(8,128)(2,1)} %param.9) | copy-start | bytes 1376260
Sparse Core Ops, SparseCore 0:
  31.9 51.9 all-gather.7
  86.2 68.2 all-gather.5
  156.2 50.4 all-gather.9
  208.8 68.2 all-gather.13
  278.7 50.4 all-gather.11
  331.5 82.0 reduce-scatter.13
  416.0 81.2 reduce-scatter.9
  499.8 81.2 reduce-scatter.11
  585.1 107.4 reduce-scatter.5
  696.3 108.9 reduce-scatter.7

commit v2 on v1

v2 whole, which is shorter than its diff:
```python
import functools

import jax
import jax.numpy as jnp
from jax import lax
from jax.experimental import pallas as pl
from jax.experimental.pallas import tpu as pltpu
from jax.sharding import Mesh
from jax.sharding import PartitionSpec as P

ROW_SPEC = P(("datb", "x", "core", "model"), None)
GATE_SPEC = P(("datb", "x", "core"), "model")
DOWN_SPEC = P("model", ("datb", "x", "core"))
BF16 = jnp.bfloat16
F32 = jnp.float32
MESH_ID = pl.DeviceIdType.MESH
RING = 4
NEAR = ((0, 0), (0, 1), (1, 0), (3, 0), (1, 1), (3, 1), (2, 0), (2, 1))
DELTAS = (0, 3, 1, 2)
LANE = 128
OUT_COLS = 512
EX, Z1, Z2, P1, P2, BL, Q1, Q2, WD = range(9)
GATHER_STEPS = (
    (Z1, 0, 0), (EX, 0, 1), (EX, 0, 2), (EX, 0, 3), (EX, 0, 4), (EX, 0, 5), (EX, 0, 6), (EX, 0, 7), (Z1, 1, 0), (BL, 0, 0), (Z1, 2, 0),
    (EX, 1, 1), (EX, 2, 1), (P1, 2, 0), (P1, 2, 1), (P1, 0, 0), (P1, 0, 1), (Z1, 0, 1), (Z1, 1, 1), (BL, 1, 0), (Z1, 2, 1), (Z2, 0, 0, 0),
    (Z1, 0, 2), (EX, 1, 2), (EX, 1, 3), (Q1, 0, 0, 0), (Q1, 0, 0, 1), (Z1, 0, 3), (EX, 1, 4), (EX, 1, 5), (Z2, 0, 0, 1), (P2, 2, 1),
    (EX, 1, 6), (EX, 1, 7), (P2, 2, 0), (Z1, 0, 4), (Q1, 1, 0, 0), (Q1, 1, 0, 1), (Z1, 0, 5), (EX, 2, 2), (EX, 2, 3), (Z1, 0, 6), (P2, 0, 0),
    (P2, 0, 1), (BL, 0, 1), (Z2, 0, 0, 2), (Z2, 0, 1, 0), (Q2, 0, 0), (EX, 2, 4), (EX, 2, 5), (Z2, 0, 0, 3), (Z2, 0, 1, 1), (EX, 2, 6),
    (EX, 2, 7), (Z1, 0, 7), (Z2, 0, 1, 2), (BL, 0, 2), (Z2, 1, 0, 0), (Q2, 1, 0), (Q1, 0, 1, 1), (P1, 1, 0), (P1, 1, 1), (Z2, 1, 0, 1),
    (Z1, 1, 2), (Z2, 0, 1, 3), (BL, 2, 1), (BL, 0, 3), (Z1, 1, 3), (Q1, 0, 2, 1), (Z1, 1, 4), (BL, 2, 2), (Z1, 1, 5), (WD, 0), (BL, 2, 0),
    (Q1, 0, 1, 0), (Z1, 1, 6), (Q1, 0, 2, 0), (Q1, 0, 3, 1), (Z1, 1, 7), (Z2, 1, 1, 0), (P2, 1, 0), (P2, 1, 1), (Z2, 1, 0, 2), (BL, 2, 3),
    (Z2, 1, 1, 1), (Q1, 2, 1, 1), (Z2, 1, 0, 3), (BL, 1, 1), (Z2, 1, 1, 2), (Q1, 2, 1, 0), (Q1, 2, 2, 0), (Q1, 2, 2, 1), (Q1, 0, 3, 0),
    (Q2, 0, 2), (Z2, 2, 0, 0), (Z2, 1, 1, 3), (BL, 1, 2), (Z2, 2, 0, 1), (Q1, 2, 0, 0), (Q1, 2, 0, 1), (Z1, 2, 2), (BL, 1, 3), (Z1, 2, 3),
    (Q2, 0, 1), (Q2, 0, 3), (Q1, 2, 3, 0), (Q1, 2, 3, 1), (Z1, 2, 4), (WD, 1),
)
CHUNK_STEPS = (
    (
        (Q2, 2, 1), (Q2, 2, 2), (Z1, 2, 5), (Q1, 1, 1, 0), (Q1, 1, 1, 1),
    ),
    (
        (Z1, 2, 6), (Q1, 1, 2, 0), (Q1, 1, 2, 1),
    ),
    (
        (Q2, 2, 0), (Q2, 2, 3), (Z2, 2, 1, 0), (Z2, 2, 0, 2), (Q1, 1, 3, 0), (Q1, 1, 3, 1), (Z1, 2, 7),
    ),
    (
        (Z2, 2, 1, 1), (Z2, 2, 1, 2), (Z2, 2, 0, 3),
    ),
    (
        (Q2, 1, 1), (Q2, 1, 2),
    ),
    (
        (Q2, 1, 3), (Z2, 2, 1, 3),
    ),
    (),
)
LATE_STEPS = (
    (WD, 2),
)
Z_ORDER = (2, 0, 1)


def dot(a, b, ca, cb):
    return lax.dot_general(a, b, (((ca,), (cb,)), ((), ())), preferred_element_type=F32)


def layer_kernel(sg, su, sd, tok, grad, tok_own, grad_own,
                 og, ou, od, out, gin, wg, wu, wd, tok_all, grad_all, h_all, ra, rb, give, rc, part, ra1, rb1, sd1, mid, ra2, rb2, sd2,
                 ff, blk, far, nxt,
                 own_sem, ex_s, ex_r, z1_s, z1_r, z2_s, z2_r, p1_s, p1_r, p2_s, p2_r, q1_s, q1_r, q2_s, q2_r, cc_s, cc_r,
                 sh_sem, wv_sem, row_sem, hst_sem, blk_sem, tmp_sem, a_s, a_r, u_s, u_r, e_s, e_r, out_sem,
                 c_s, c_r, a1_s, a1_r, f1_s, f1_r, d1_s, d1_r, a2_s, a2_r, f2_s, f2_r, d2_s, d2_r):
    z, y = lax.axis_index("datb"), lax.axis_index("model")
    x, core = lax.axis_index("x"), lax.axis_index("core")
    i8 = 2 * x + core
    n8 = 2 * RING
    rows, d = tok.shape
    half_rows = rows // 2
    chunk = RING * rows
    n_chunk = n8
    nf, tokens = ff.shape[1:]
    dp = sg.shape[0]
    half = nf // 2
    cols = blk.shape[2]
    tiles = far.shape[1] // LANE
    outs = (og, ou, od)

    zs, ys, xs = ([v] + [lax.rem(v + k, RING) for k in range(1, RING)] for v in (z, y, x))
    cores = (core, 1 - core)
    peers = [[2 * v + c for c in cores] for v in xs]
    slot_at = [[[pl.multiple_of((zz * n8 + peers[dx][dc]) * dp, 16) for dc in range(2)] for dx in range(RING)] for zz in zs]
    hand_at = [[pl.multiple_of(p * dp, 8) for p in row] for row in peers]
    rows_at = [[[pl.multiple_of((peers[dx][dc] * RING + yy) * rows, half_rows) for dc in range(2)] for yy in ys] for dx in range(RING)]
    lanes_at = [pl.multiple_of(zz * cols, LANE) for zz in zs]

    def peer(dx, dc):
        return peers[dx][dc]

    def zdev(k):
        return {"datb": zs[k]}

    def xdev(k):
        return {"x": xs[k]}

    def ydev(k):
        return {"model": ys[k]}

    def near(dx, dc):
        return {"x": xs[dx], "core": cores[dc]}

    def copy(src, dst, s, r, dev):
        return pltpu.make_async_remote_copy(src_ref=src, dst_ref=dst, send_sem=s, recv_sem=r, device_id=dev, device_id_type=MESH_ID)

    rcopy = copy

    def start(copies):
        for c in copies:
            c.start()

    def received(copies):
        for c in copies:
            c.wait_recv()

    def sent(copies):
        for c in copies:
            c.wait_send()

    barrier = pltpu.get_barrier_semaphore()
    others = [zdev(1), zdev(3), ydev(1), ydev(3)] + [near(*n) for n in NEAR[1:]]
    for dev in others:
        pl.semaphore_signal(barrier, inc=1, device_id=dev, device_id_type=MESH_ID)

    def blk_load(t, slot, k):
        src = tok_all if t < 2 else grad_all
        return pltpu.make_async_copy(src.at[:, pl.ds(lanes_at[k], cols)], blk.at[slot], blk_sem.at[slot])

    def product(t, slot, dst):
        step = 2 * LANE

        def one(n, carry):
            lanes = pl.ds(pl.multiple_of(jnp.minimum(n * step, cols - step), LANE), step)
            dst[:nf, lanes] = jnp.dot(ff[t], blk[slot, :, lanes], preferred_element_type=F32)
            return carry

        lax.fori_loop(0, -(-cols // step), one, 0)

    lo, hi = pl.ds(0, half), pl.ds(half, half)

    def a_copies(t):
        return [rcopy(far.at[t, rows], ra.at[t, rows], a_s.at[t, s], a_r.at[t, s], zdev(k)) for s, rows, k in ((0, lo, 1), (1, hi, 3))]

    def tile_rows(tile):
        return pl.ds(tile * LANE, min(LANE, nf - tile * LANE))

    def unit_copies(t, tile):
        at = tile_rows(tile)
        return [rcopy(nxt.at[t, s, at], rb.at[t, s, at], u_s.at[t, s, tile], u_r.at[t, s, tile], zdev(1 + 2 * s)) for s in range(2)]

    def far_block(t):
        blk_load(t, 0, 2).start()
        blk_load(t, 0, 2).wait()
        product(t, 0, far.at[t])
        start(a_copies(t))

    def forward_phase(shard, pieces, wv, rowbuf, av, bv, hst):
        fulls = (wg, wu, wd)
        loads = [pltpu.make_async_copy(src, shard.at[t], sh_sem.at[t]) for t, src in enumerate((sg, su, sd))]
        for c in loads:
            c.start()

        def cut_pieces(t):
            loads[t].wait()
            for j in range(n8):
                pieces[t, j] = shard[t, :, j * nf:(j + 1) * nf]

        started = []

        def go(make, *args):
            make(*args).start()
            started.append((make, args))

        def slot(t, k, source):
            dx, dc = source
            return fulls[t].at[pl.ds(slot_at[k][dx][dc], dp)]

        def source(k):
            dx, dc = NEAR[k]
            return (RING - dx) % RING, dc

        def back(side):
            return 3 if side == 0 else 1

        def ahead(side):
            return 1 if side == 0 else 3

        def exchange_copy(t, k):
            return copy(pieces.at[t, peer(*NEAR[k])], slot(t, 0, NEAR[0]), ex_s.at[t, k], ex_r.at[t, k], near(*NEAR[k]))

        def exchange(t, k):
            go(exchange_copy, t, k)

        def z_first_copy(t, side, k):
            here = slot(t, 0, source(k))
            return copy(here if k else pieces.at[t, i8], here, z1_s.at[t, side, k], z1_r.at[t, side, k], zdev(ahead(side)))

        def z_first(t, k):
            if k:
                here = slot(t, 0, source(k))
                copy(here, here, ex_s.at[t, k], ex_r.at[t, k], {"datb": z}).wait_recv()
            for side in range(2):
                go(z_first_copy, t, side, k)

        def wait_z_first(t, side, k):
            there = slot(t, back(side), source(k))
            copy(there, there, z1_s.at[t, side, k], z1_r.at[t, side, k], {"datb": z}).wait_recv()

        def z_second_copy(t, side, k):
            there = slot(t, back(side), source(k + side * (n8 // 2)))
            return copy(there, there, z2_s.at[t, side, k], z2_r.at[t, side, k], zdev(ahead(side)))

        def z_second(t, side, k):
            wait_z_first(t, side, k + side * (n8 // 2))
            go(z_second_copy, t, side, k)

        def weights_done(t):
            local[t].wait()
            for k in range(n8 // 2):
                wait_z_first(t, 0, n8 // 2 + k)
                wait_z_first(t, 1, k)
                for side in range(2):
                    there = slot(t, 2, source(k + side * (n8 // 2)))
                    copy(there, there, z2_s.at[t, side, k], z2_r.at[t, side, k], {"datb": z}).wait_recv()
            w_load(t).start()

        cut = d // 2
        rings = ((tok, tok_all, pl.ds(0, d), True), (grad, grad_all, pl.ds(0, cut), True), (grad, grad_all, pl.ds(cut, d - cut), False))

        def axis(r, n):
            return xdev if rings[r][3] == (n == 1) else ydev

        def block(r, da, db, flip=0, lo=0, size=rows):
            dx, dy = (da, db) if rings[r][3] else (db, da)
            first = rows_at[dx][dy][flip]
            return rings[r][1].at[pl.ds(pl.multiple_of(first + lo, half_rows) if lo else first, size), rings[r][2]]

        def own_block(r):
            return rings[r][0].at[:, rings[r][2]]

        def to_core_copy(r, ia, ib):
            there = block(r, DELTAS[ia], DELTAS[ib])
            return copy(own_block(r) if ia == 0 and ib == 0 else there, there, cc_s.at[r, ia, ib], cc_r.at[r, ia, ib], near(0, 1))

        def to_core(r, ia, ib):
            go(to_core_copy, r, ia, ib)

        def first_copy(r, side):
            return copy(own_block(r), block(r, 0, 0), p1_s.at[r, side], p1_r.at[r, side], axis(r, 1)(ahead(side)))

        def first_own(r, side):
            go(first_copy, r, side)

        def first_far_copy(r, side):
            part = block(r, back(side), 0, 0, side * half_rows, half_rows)
            return copy(part, part, p2_s.at[r, side], p2_r.at[r, side], axis(r, 1)(ahead(side)))

        def first_forward(r, side):
            there = block(r, back(side), 0)
            copy(there, there, p1_s.at[r, side], p1_r.at[r, side], {"datb": z}).wait_recv()
            go(first_far_copy, r, side)

        def block_on(r, ia):
            for side in range(2 if ia == 3 else 0):
                part = block(r, 2, 0, 0, side * half_rows, half_rows)
                copy(part, part, p2_s.at[r, side], p2_r.at[r, side], {"datb": z}).wait_recv()
            for side in range(2):
                go(second_copy, r, side, ia)
            to_core(r, ia, 0)

        def second_copy(r, side, ia):
            there = block(r, DELTAS[ia], 0)
            return copy(there if ia else own_block(r), there, q1_s.at[r, side, ia], q1_r.at[r, side, ia], axis(r, 2)(ahead(side)))

        def second_far_copy(r, ia):
            side = ia // 2
            there = block(r, DELTAS[ia], back(side))
            return copy(there, there, q2_s.at[r, ia], q2_r.at[r, ia], axis(r, 2)(ahead(side)))

        def second_forward(r, ia, side):
            there = block(r, DELTAS[ia], back(side))
            copy(there, there, q1_s.at[r, side, ia], q1_r.at[r, side, ia], {"datb": z}).wait_recv()
            if ia // 2 == side:
                go(second_far_copy, r, ia)
            to_core(r, ia, 1 if side == 0 else 2)

        def second_far(r, ia):
            there = block(r, DELTAS[ia], 2)
            copy(there, there, q2_s.at[r, ia], q2_r.at[r, ia], {"datb": z}).wait_recv()
            to_core(r, ia, 3)

        def rows_in(r):
            for ia in range(RING):
                for ib in range(RING):
                    there = block(r, DELTAS[ia], DELTAS[ib], 1)
                    copy(there, there, cc_s.at[r, ia, ib], cc_r.at[r, ia, ib], {"datb": z}).wait_recv()

        local = [pltpu.make_async_copy(pieces.at[t, i8], slot(t, 0, NEAR[0]), own_sem.at[t]) for t in range(3)]
        local += [pltpu.make_async_copy(own_block(r), block(r, 0, 0), own_sem.at[3 + r]) for r in range(3)]

        def w_load(t):
            return pltpu.make_async_copy(fulls[t], wv.at[t % 2], wv_sem.at[t])

        def row_load(src, i, buf):
            return pltpu.make_async_copy(src.at[chunk_rows(i)], rowbuf.at[buf], row_sem.at[buf])

        def chunk_loop(src, work, between):
            row_load(src, 0, 0).start()

            def outer(xx, carry):
                def inner(c, carry):
                    i = 2 * xx + c

                    @pl.when(i + 1 < n_chunk)
                    def _():
                        row_load(src, i + 1, 1 - c).start()

                    for k, step in enumerate(between):
                        pl.when(i == k)(step)
                    row_load(src, i, c).wait()
                    work(i, xx, c)
                    return carry

                return lax.fori_loop(0, 2, inner, carry)

            lax.fori_loop(0, RING, outer, 0)

        def chunk_rows(i):
            return pl.ds(pl.multiple_of(i * chunk, chunk), chunk)

        def h_copy(xx, c, slot, j):
            return pltpu.make_async_copy(hst.at[c, slot], h_all.at[j, xx, c], hst_sem.at[c, slot])

        def keep(i, xx, c, slot, j, value):
            @pl.when(xx >= 1)
            def _():
                h_copy(xx - 1, c, slot, j).wait()

            hst[c, slot] = value.astype(BF16)
            h_copy(xx, c, slot, j).start()
            ff[j, :, chunk_rows(i)] = value.T.astype(BF16)

        def kept(slot, j):
            for c in range(2):
                h_copy(RING - 1, c, slot, j).wait()

        def pre_work(i, xx, c):
            rb_ = rowbuf[c]
            a = jnp.dot(rb_, wv[0], preferred_element_type=F32).astype(BF16)
            b = jnp.dot(rb_, wv[1], preferred_element_type=F32).astype(BF16)
            av[chunk_rows(i)] = a
            bv[chunk_rows(i)] = b
            a, b = a.astype(F32), b.astype(F32)
            keep(i, xx, c, 0, 2, a * jax.nn.sigmoid(a) * b)

        def post_work(i, xx, c):
            g = jnp.dot(rowbuf[c], wv[0], preferred_element_type=F32).astype(BF16).astype(F32)
            a, b = av[chunk_rows(i)].astype(F32), bv[chunk_rows(i)].astype(F32)
            sig = jax.nn.sigmoid(a)
            keep(i, xx, c, 0, 0, g * b * sig * (1.0 + a * (1.0 - sig)))
            keep(i, xx, c, 1, 1, g * (a * sig))

        steps = (exchange, z_first, z_second, first_own, first_forward, block_on, second_forward, second_far, weights_done)

        def run(group):
            for which, *args in group:
                steps[which](*args)

        with jax.named_scope("begin"):
            for t in range(3):
                cut_pieces(t)
            pl.semaphore_wait(barrier, len(others))
            for c in local:
                c.start()
        with jax.named_scope("gather"):
            run(GATHER_STEPS)
            local[3].wait()
            rows_in(0)
            w_load(0).wait()
            w_load(1).wait()
        with jax.named_scope("gate_up"):
            chunk_loop(tok_all, pre_work, [functools.partial(run, group) for group in CHUNK_STEPS])
            kept(0, 2)
        with jax.named_scope("rows"):
            for r in (1, 2):
                local[3 + r].wait()
                rows_in(r)
        far_block(2)
        with jax.named_scope("late"):
            run(LATE_STEPS)
            w_load(2).wait()
        with jax.named_scope("down"):
            chunk_loop(grad_all, post_work, ())
            kept(0, 0)
            kept(1, 1)
        for make, args in started:
            make(*args).wait_send()

    def backward_phase(tmp, stage):
        def next_blocks(t):
            for s in range(2):
                blk_load(t, s, 1 + 2 * s).start()
            for s in range(2):
                blk_load(t, s, 1 + 2 * s).wait()
                product(t, s, nxt.at[t, s])
            received(a_copies(t))
            cs = [pltpu.make_async_copy(ra.at[t, rows], tmp.at[s, rows], tmp_sem.at[s]) for s, rows in ((0, lo), (1, hi))]
            start(cs)
            for c, (s, rows) in zip(cs, ((0, lo), (1, hi))):
                c.wait()
                nxt[t, s, rows] += tmp[s, rows]
            for tile in range(tiles):
                start(unit_copies(t, tile))

        def own_block(t):
            blk_load(t, 0, 0).start()
            sent(a_copies(t))
            blk_load(t, 0, 0).wait()
            product(t, 0, far.at[t])

        def slot(t):
            return Z_ORDER.index(t) % 2

        def hand_out(t, tile):
            lanes = pl.ds(tile * LANE, LANE)
            cs = []
            for k in range(1, n8):
                at = pl.ds(hand_at[NEAR[k][0]][NEAR[k][1]], dp)
                cs.append(rcopy(stage.at[slot(t), at, lanes], outs[t].at[i8, :, lanes], e_s.at[t, tile, k], e_r.at[t, tile, k], near(*NEAR[k])))
            at = pl.ds(hand_at[0][0], dp)
            return cs, pltpu.make_async_copy(stage.at[slot(t), at, lanes], outs[t].at[i8, :, lanes], out_sem.at[t, tile])

        def handed(t, tile):
            cs, mine = hand_out(t, tile)
            sent(cs)
            mine.wait()

        def finish(t, tile):
            received(unit_copies(t, tile))
            at = tile_rows(tile)
            cs = [pltpu.make_async_copy(rb.at[t, s, at], tmp.at[s, at], tmp_sem.at[s]) for s in range(2)]
            start(cs)
            if t == Z_ORDER[2]:
                handed(Z_ORDER[0], tile)
            for c in cs:
                c.wait()
            wide = pl.ds(tile * LANE, LANE)
            stage[slot(t), :, wide] = (far[t, wide] + tmp[0, wide] + tmp[1, wide]).T
            cs, mine = hand_out(t, tile)
            start(cs + [mine])

        blocks = d // min(OUT_COLS, d)
        width = d // blocks

        def row_products(r, keep):
            side = core if keep else 1 - core
            terms = ((2, wd),) if r == 0 else ((0, wg), (1, wu))
            specs, args = [], []
            for t, w in terms:
                specs += [pl.BlockSpec((1, RING, 1, RING * rows, nf), lambda j, t=t: (t, 0, side, 0, 0)), pl.BlockSpec((width, nf), lambda j: (j, 0))]
                args += [h_all, w]
            wide = pl.BlockSpec((RING, RING, rows, width), lambda j: (0, 0, 0, j))
            if keep:
                specs.append(wide)
                args.append(rc.at[r])

            def body(*refs):
                total = None
                for i in range(len(terms)):
                    h = refs[2 * i][...].reshape(RING * RING * rows, nf)
                    prod = dot(h, refs[2 * i + 1][...], 1, 1)
                    total = prod if total is None else total + prod
                if keep:
                    total = total + refs[-2][...].astype(F32).reshape(total.shape)
                refs[-1][...] = total.astype(BF16).reshape(RING, RING, rows, width)

            pltpu.emit_pipeline(body, grid=(blocks,), in_specs=specs, out_specs=[wide])(*args, (part if keep else give).at[r])

        def core_copy(r):
            return rcopy(give.at[r], rc.at[r], c_s.at[r], c_r.at[r], near(0, 1))

        def level(n):
            if n == 1:
                def piece(r, k, h):
                    return part.at[r, pl.ds(2 * h, 2), ys[k]]
                return ydev, piece, ra1, rb1, sd1, (a1_s, a1_r, f1_s, f1_r, d1_s, d1_r)

            def piece(r, k, h):
                return mid.at[r, xs[k], pl.ds(h, 1)]
            return xdev, piece, ra2, rb2, sd2, (a2_s, a2_r, f2_s, f2_r, d2_s, d2_r)

        def ring_a(r, n):
            dev, piece, rfar, _, _, sems = level(n)
            return [rcopy(piece(r, 2, s), rfar.at[r, s], sems[0].at[r, s], sems[1].at[r, s], dev(1 + 2 * s)) for s in range(2)]

        def ring_f(r, n):
            dev, piece, _, rnear, _, sems = level(n)
            return [rcopy(piece(r, 1 + 2 * s, 1 - s), rnear.at[r, s, 1 - s], sems[2].at[r, s], sems[3].at[r, s], dev(1 + 2 * s)) for s in range(2)]

        def ring_d(r, n):
            dev, _, _, rnear, dep, sems = level(n)
            return [rcopy(dep.at[r, s], rnear.at[r, s, s], sems[4].at[r, s], sems[5].at[r, s], dev(1 + 2 * s)) for s in range(2)]

        def add(grid, *terms):
            specs = []
            for ref, at, lead in terms:
                tail = ref.shape[lead:]
                specs.append(pl.BlockSpec((1,) * lead + tuple(tail), lambda *i, at=at, rank=len(tail): tuple(at(*i)) + (0,) * rank))

            def body(*refs):
                total = refs[0][...].astype(F32).reshape(refs[0].shape[-2:])
                for ref in refs[1:-1]:
                    total = total + ref[...].astype(F32).reshape(total.shape)
                refs[-1][...] = total.astype(BF16).reshape(refs[-1].shape)

            pltpu.emit_pipeline(body, grid=grid, in_specs=specs[:-1], out_specs=specs[-1:])(*[ref for ref, _, _ in terms])

        def ring_first(r, n):
            start(ring_a(r, n) + ring_f(r, n))

        def ring_dependent(r, n):
            received(ring_a(r, n))
            if n == 1:
                add((2, 2), (part.at[r], lambda s, i: (2 * s + i, lax.rem(y + 1 + 2 * s, RING)), 2), (ra1.at[r], lambda s, i: (s, i), 2),
                    (sd1.at[r], lambda s, i: (s, i), 2))
            else:
                add((2,), (mid.at[r], lambda s: (lax.rem(x + 1 + 2 * s, RING), s), 2), (ra2.at[r], lambda s: (s, 0), 2),
                    (sd2.at[r], lambda s: (s, 0), 2))
            start(ring_d(r, n))

        def ring_last(r, n):
            received(ring_f(r, n) + ring_d(r, n))
            if n == 1:
                add((2, 2), (part.at[r], lambda h, i: (2 * h + i, y), 2), (rb1.at[r, 0], lambda h, i: (h, i), 2),
                    (rb1.at[r, 1], lambda h, i: (h, i), 2), (mid.at[r], lambda h, i: (2 * h + i,), 1))
            else:
                own, res = ((tok_own, out), (grad_own, gin))[r]
                add((2,), (own, lambda h: (h,), 1), (mid.at[r], lambda h: (x, h), 2), (rb2.at[r, 0], lambda h: (h, 0), 2),
                    (rb2.at[r, 1], lambda h: (h, 0), 2), (res, lambda h: (h,), 1))

        def give_rows(r):
            row_products(r, False)
            core_copy(r).start()

        def keep_rows(r):
            core_copy(r).wait_recv()
            row_products(r, True)

        order = [
            (far_block, 0), (give_rows, 0), (next_blocks, 2), (far_block, 1), (own_block, 2), (keep_rows, 0), (ring_first, 0, 1),
            (finish, 2, 0), (give_rows, 1), (finish, 2, 1), (finish, 2, 2), (next_blocks, 0), (finish, 2, 3), (ring_dependent, 0, 1),
            (finish, 2, 4), (own_block, 0), (keep_rows, 1), (ring_first, 1, 1), (next_blocks, 1), (ring_last, 0, 1), (ring_first, 0, 2),
            (finish, 0, 0), (own_block, 1), (finish, 0, 1), (ring_dependent, 0, 2), (ring_dependent, 1, 1), (finish, 0, 2), (finish, 0, 3),
            (ring_last, 0, 2), (finish, 0, 4), (finish, 1, 0), (finish, 1, 1), (ring_last, 1, 1), (ring_first, 1, 2), (finish, 1, 2),
            (ring_dependent, 1, 2), (finish, 1, 3), (finish, 1, 4), (ring_last, 1, 2),
        ]
        for fn, *args in order:
            with jax.named_scope("_".join(str(v) for v in [fn.__name__, *args])):
                fn(*args)

        for t in range(3):
            for tile in range(tiles):
                sent(unit_copies(t, tile))
                received(hand_out(t, tile)[0])
                if t != Z_ORDER[0]:
                    handed(t, tile)
        for r in range(2):
            core_copy(r).wait_send()
            for n in (1, 2):
                sent(ring_a(r, n) + ring_f(r, n) + ring_d(r, n))

    pl.run_scoped(
        forward_phase,
        pltpu.VMEM((3,) + sg.shape, BF16),
        pltpu.VMEM((3, n8, dp, nf), BF16),
        pltpu.VMEM((2, d, nf), BF16),
        pltpu.VMEM((2, chunk, d), BF16),
        pltpu.VMEM((tokens, nf), BF16),
        pltpu.VMEM((tokens, nf), BF16),
        pltpu.VMEM((2, 2, chunk, nf), BF16),
    )
    pl.run_scoped(backward_phase, pltpu.VMEM((2, tiles * LANE, cols), F32), pltpu.VMEM((2, cols, tiles * LANE), F32))


def layer(sg, su, sd, tok, grad):
    n8 = 2 * RING
    dp, nf = sg.shape[0], sg.shape[1] // n8
    rows, d = tok.shape
    tokens = rows * RING * n8
    cols = d // RING
    tiles = -(-nf // LANE)
    padded = tiles * LANE
    hbm = pl.BlockSpec(memory_space=pl.ANY)
    dma = pltpu.SemaphoreType.DMA
    sds = jax.ShapeDtypeStruct
    halves = (2, rows // 2, d)
    res = pl.pallas_call(
        layer_kernel,
        out_shape=[sds((n8, dp, padded), F32)] * 3 + [sds(halves, BF16)] * 2 + [
            sds((d, nf), BF16), sds((d, nf), BF16), sds((d, nf), BF16), sds((tokens, d), BF16), sds((tokens, d), BF16),
            sds((3, RING, 2, RING * rows, nf), BF16),
            sds((3, nf, cols), F32), sds((3, 2, nf, cols), F32),
            sds((2, RING, RING, rows, d), BF16), sds((2, RING, RING, rows, d), BF16), sds((2, RING, RING, rows, d), BF16),
            sds((2, 2, 2, rows, d), BF16), sds((2, 2, 2, 2, rows, d), BF16), sds((2, 2, 2, rows, d), BF16),
            sds((2, RING, 2, rows // 2, d), BF16),
            sds((2, 2, 1, rows // 2, d), BF16), sds((2, 2, 2, 1, rows // 2, d), BF16), sds((2, 2, 1, rows // 2, d), BF16),
        ],
        in_specs=[hbm] * 7,
        out_specs=[hbm] * 23,
        scratch_shapes=[
            pltpu.VMEM((3, nf, tokens), BF16),
            pltpu.VMEM((2, tokens, cols), BF16),
            pltpu.VMEM((3, padded, cols), F32),
            pltpu.VMEM((3, 2, nf, cols), F32),
            dma((6,)),
            dma((3, n8)), dma((3, n8)),
            dma((3, 2, n8)), dma((3, 2, n8)),
            dma((3, 2, n8 // 2)), dma((3, 2, n8 // 2)),
            dma((3, 2)), dma((3, 2)),
            dma((3, 2)), dma((3, 2)),
            dma((3, 2, RING)), dma((3, 2, RING)),
            dma((3, RING)), dma((3, RING)),
            dma((3, RING, RING)), dma((3, RING, RING)),
            dma((3,)), dma((3,)), dma((2,)), dma((2, 2)), dma((2,)), dma((2,)),
            dma((3, 2)), dma((3, 2)),
            dma((3, 2, tiles)), dma((3, 2, tiles)),
            dma((3, tiles, n8)), dma((3, tiles, n8)),
            dma((3, tiles)),
            dma((2,)), dma((2,)),
        ] + [dma((2, 2))] * 12,
        compiler_params=pltpu.CompilerParams(collective_id=0, has_side_effects=True, vmem_limit_bytes=67043328),
        cost_estimate=pl.CostEstimate(flops=18 * nf * tokens * d, bytes_accessed=300_000_000, transcendentals=0),
        name="layer",
    )(sg, su, sd, tok, grad, tok.reshape(halves), grad.reshape(halves))
    return res[:3], res[3].reshape(rows, d), res[4].reshape(rows, d)


def assemble_kernel(og, ou, od, out, gin, g, u, w, res, gres, buf, flat, in_sem, out_sem, row_buf, row_sem):
    n8, nf = og.shape[0], g.shape[1] // og.shape[0]
    srcs, dsts = (og, ou, od), (g, u, w)
    rows_in = [pltpu.make_async_copy(src, row_buf.at[r], row_sem.at[r]) for r, src in enumerate((out, gin))]
    loads = [pltpu.make_async_copy(src, buf.at[t], in_sem.at[t]) for t, src in enumerate(srcs)]
    stores = [pltpu.make_async_copy(flat.at[t], dst, out_sem.at[t]) for t, dst in enumerate(dsts)]
    for c in loads + rows_in:
        c.start()
    for t in range(3):
        loads[t].wait()
        for j in range(n8):
            flat[t, :, j * nf:(j + 1) * nf] = buf[t, j, :, :nf]
        stores[t].start()
    rows_out = [pltpu.make_async_copy(row_buf.at[r], dst, row_sem.at[r]) for r, dst in enumerate((res, gres))]
    for c in rows_in:
        c.wait()
    for c in rows_out:
        c.start()
    for c in stores + rows_out:
        c.wait()


def assemble(sums, out, gin, ff):
    n8, dp, padded = sums[0].shape
    hbm = pl.BlockSpec(memory_space=pl.ANY)
    dma = pltpu.SemaphoreType.DMA
    sds = jax.ShapeDtypeStruct
    return pl.pallas_call(
        assemble_kernel,
        out_shape=[sds((dp, ff), F32)] * 3 + [sds(out.shape, BF16)] * 2,
        in_specs=[hbm] * 5,
        out_specs=[hbm] * 5,
        scratch_shapes=[
            pltpu.VMEM((3, n8, dp, padded), F32), pltpu.VMEM((3, dp, ff), F32), dma((3,)), dma((3,)),
            pltpu.VMEM((2,) + out.shape, BF16), dma((2,)),
        ],
        compiler_params=pltpu.CompilerParams(vmem_limit_bytes=63 * 1024 * 1024),
        name="assemble",
    )(*sums, out, gin)


def solution(mesh):
    nz, ny, nd = mesh.shape["datb"], mesh.shape["model"], mesh.shape["data"]
    fine = Mesh(mesh.devices.reshape(nz, ny, nd // 2, 2), ("datb", "model", "x", "core"))

    def local_step(tok_loc, wg_loc, wu_loc, wd_loc, grad_loc):
        sums, out, grad_in = layer(wg_loc, wu_loc, wd_loc.T, tok_loc, grad_loc)
        grad_gate, grad_up, grad_down_t, out, grad_in = assemble(sums, out, grad_in, wg_loc.shape[1])
        return out, grad_in, grad_gate, grad_up, grad_down_t.T

    return jax.shard_map(local_step, mesh=fine, in_specs=(ROW_SPEC, GATE_SPEC, GATE_SPEC, DOWN_SPEC, ROW_SPEC), out_specs=(ROW_SPEC, ROW_SPEC, GATE_SPEC, GATE_SPEC, DOWN_SPEC), check_vma=False)
```

time: 819 us -> 369 us (0.45)
  waiting for transfers between devices: 531 us -> 0 us
  Pallas kernels: 0 us -> 366 us
  matrix products: 158 us -> 0 us
  blocking collectives: 61.8 us -> 0 us
  local copies, waits for them, and re-layouts: 28.7 us -> 0 us
  starting transfers between devices: 16.7 us -> 0 us
  between operations: 14.5 us -> 0.82 us
    pallas_call x0 -> x2, Pallas kernels: none -> 366 us  [the longest x1 361 us: layer(): pl.pallas_call(layer_kernel, out_shape=[sds((n8, dp, padded), F32)] * 3 +...]
    reduce_scatter x5 -> x0, waiting for transfers between devices: 304 us -> none  [the longest x2 181 us: to_rows(): lax.psum_scatter(part, ('data', 'model'), scatter_dimension=0, tiled=True)]
    all_gather x5 -> x0, waiting for transfers between devices: 207 us -> none  [the longest x1 70.6 us: local_step(): tok = lax.all_gather(tok_loc, ('data', 'model'), axis=0, tiled=True)]
    dot_general x9 -> x0, matrix products: 158 us -> none  [the longest x1 21.9 us: local_step(): jnp.dot(dgate, wg.T, preferred_element_type=jnp.float32)]
    all_to_all x3 -> x0, blocking collectives: 61.8 us -> none  [the longest x2 41.8 us: gate_like(): w = lax.all_to_all(w, 'data', 1, 0, tiled=True)]
    all_to_all x12 -> x0, local copies, waits for them, and re-layouts: 19.4 us -> none  [the longest x4 8.25 us: grad_gate_like(): return lax.all_to_all(g, 'data', 0, 1, tiled=True)]
    all_to_all x3 -> x0, waiting for transfers between devices: 19 us -> none  [the longest x2 19 us: grad_gate_like(): return lax.all_to_all(g, 'data', 0, 1, tiled=True)]
    all_to_all x3 -> x0, starting transfers between devices: 15.8 us -> none  [the longest x2 10.6 us: grad_gate_like(): return lax.all_to_all(g, 'data', 0, 1, tiled=True)]
  transfers between devices with their start and end apart: 13 -> 0, of which waited for: 10 -> 0; matrix products, arithmetic and copies ran while one was open for 22% -> 0% of each run, Pallas kernels for 0% -> 0%
where the time goes in v2:
time: 369 us; the launch traced here: 367 us
  Pallas kernels  366 us (99%)
    pallas_call x1, Pallas kernels, layer(): pl.pallas_call(layer_kernel, out_shape=[sds((n8, dp, padded), F32)] * 3 +...  361 us

profile of v2, /device:TPU:1, one launch (start us, length us, event | category | flops | bytes accessed | tf_op | source)
XLA Modules:
  0.0 366.9 jit_solution(13869354908692952576)
XLA Ops:
  0.6 360.7 %layer.1 = (f32[8,112,640]{2,1,0:T(8,128)}, f32[8,112,640]{2,1,0:T(8,128)}, f32[8,112,640]{2,1,0:T(8,128)}, bf16[2,32,3584]{2,1,0:T(8,128)(2,1)}, bf16[2,32,3584...) custom-call(bf16[112,4736]{1,0:T(8,128)(2,1)} %sg.1, ...), custom_call_target="tpu_custom_call" | custom-call | flops 78215380992 | bytes 300000000 | tf_op jit(solution)/shard_map/layer/pallas_call | solution.py:605
  361.3 5.4 %assemble.1 = (f32[112,4736]{1,0:T(8,128)}, f32[112,4736]{1,0:T(8,128)}, f32[112,4736]{1,0:T(8,128)}, bf16[64,3584]{1,0:T(8,128)(2,1)}, bf16[64,3584]{1,0:T(8,128)(2,1)}) custom-call(f32[8,112,640]{2,1,0:T(8,128)} %get-tuple-element.15.og, f32[8,112,640]{2,1,0:T(8,128)} %get-tuple-element.16.ou, f32[8,112,640]{2,1,0:T(8,128)} %get-tuple-element.17.od, ...), custom_call_target="tpu_custom_call" | custom-call | tf_op jit(solution)/shard_map/assemble/pallas_call | solution.py:673

commit v3 on v2

--- a/solution.py
+++ b/solution.py
@@ -19,38 +19,63 @@
 DELTAS = (0, 3, 1, 2)
 LANE = 128
 OUT_COLS = 512
-EX, Z1, Z2, P1, P2, BL, Q1, Q2, WD = range(9)
+EX, Z1, Z2, P1, P2, BL, Q1, Q2, WD, CI = range(10)
 GATHER_STEPS = (
-    (Z1, 0, 0), (EX, 0, 1), (EX, 0, 2), (EX, 0, 3), (EX, 0, 4), (EX, 0, 5), (EX, 0, 6), (EX, 0, 7), (Z1, 1, 0), (BL, 0, 0), (Z1, 2, 0),
-    (EX, 1, 1), (EX, 2, 1), (P1, 2, 0), (P1, 2, 1), (P1, 0, 0), (P1, 0, 1), (Z1, 0, 1), (Z1, 1, 1), (BL, 1, 0), (Z1, 2, 1), (Z2, 0, 0, 0),
-    (Z1, 0, 2), (EX, 1, 2), (EX, 1, 3), (Q1, 0, 0, 0), (Q1, 0, 0, 1), (Z1, 0, 3), (EX, 1, 4), (EX, 1, 5), (Z2, 0, 0, 1), (P2, 2, 1),
-    (EX, 1, 6), (EX, 1, 7), (P2, 2, 0), (Z1, 0, 4), (Q1, 1, 0, 0), (Q1, 1, 0, 1), (Z1, 0, 5), (EX, 2, 2), (EX, 2, 3), (Z1, 0, 6), (P2, 0, 0),
-    (P2, 0, 1), (BL, 0, 1), (Z2, 0, 0, 2), (Z2, 0, 1, 0), (Q2, 0, 0), (EX, 2, 4), (EX, 2, 5), (Z2, 0, 0, 3), (Z2, 0, 1, 1), (EX, 2, 6),
-    (EX, 2, 7), (Z1, 0, 7), (Z2, 0, 1, 2), (BL, 0, 2), (Z2, 1, 0, 0), (Q2, 1, 0), (Q1, 0, 1, 1), (P1, 1, 0), (P1, 1, 1), (Z2, 1, 0, 1),
-    (Z1, 1, 2), (Z2, 0, 1, 3), (BL, 2, 1), (BL, 0, 3), (Z1, 1, 3), (Q1, 0, 2, 1), (Z1, 1, 4), (BL, 2, 2), (Z1, 1, 5), (WD, 0), (BL, 2, 0),
-    (Q1, 0, 1, 0), (Z1, 1, 6), (Q1, 0, 2, 0), (Q1, 0, 3, 1), (Z1, 1, 7), (Z2, 1, 1, 0), (P2, 1, 0), (P2, 1, 1), (Z2, 1, 0, 2), (BL, 2, 3),
-    (Z2, 1, 1, 1), (Q1, 2, 1, 1), (Z2, 1, 0, 3), (BL, 1, 1), (Z2, 1, 1, 2), (Q1, 2, 1, 0), (Q1, 2, 2, 0), (Q1, 2, 2, 1), (Q1, 0, 3, 0),
-    (Q2, 0, 2), (Z2, 2, 0, 0), (Z2, 1, 1, 3), (BL, 1, 2), (Z2, 2, 0, 1), (Q1, 2, 0, 0), (Q1, 2, 0, 1), (Z1, 2, 2), (BL, 1, 3), (Z1, 2, 3),
-    (Q2, 0, 1), (Q2, 0, 3), (Q1, 2, 3, 0), (Q1, 2, 3, 1), (Z1, 2, 4), (WD, 1),
+    (Z1, 0, 0), (Z1, 1, 0), (P1, 0, 0), (P1, 0, 1), (EX, 0, 1), (EX, 0, 2), (EX, 0, 3), (Z1, 2, 0), (EX, 1, 1), (BL, 0, 0), (EX, 2, 1),
+    (P1, 2, 0), (P1, 2, 1), (EX, 0, 4), (EX, 0, 5), (Z1, 0, 1), (Z1, 1, 1), (BL, 1, 0), (Z1, 2, 1), (EX, 0, 6), (EX, 0, 7), (Z2, 0, 0, 0),
+    (Z2, 1, 0, 0), (EX, 1, 2), (EX, 1, 3), (Z2, 2, 0, 0), (Q1, 0, 0, 0), (Q1, 0, 0, 1), (EX, 1, 4), (EX, 1, 5), (Z1, 0, 2), (EX, 1, 6),
+    (EX, 1, 7), (P2, 2, 1), (P2, 2, 0), (Z1, 0, 3), (Z1, 0, 4), (P2, 0, 0), (P2, 0, 1), (BL, 0, 1), (Q1, 1, 0, 1), (Z1, 0, 5), (EX, 2, 2),
+    (EX, 2, 3), (Z1, 0, 6), (Z2, 0, 1, 0), (BL, 0, 2), (EX, 2, 4), (EX, 2, 5), (Z1, 0, 7), (Q2, 0, 0), (Z2, 0, 1, 1), (EX, 2, 6),
+    (EX, 2, 7), (Z2, 0, 0, 1), (Q1, 0, 1, 1), (Z2, 0, 1, 2), (Z2, 0, 0, 2), (P1, 1, 0), (P1, 1, 1), (Q1, 1, 0, 0), (Z2, 0, 0, 3),
+    (Z2, 0, 1, 3), (Z1, 1, 2), (BL, 2, 1), (Q1, 0, 2, 1), (Q1, 0, 1, 0), (Z1, 1, 3), (Z1, 1, 4), (BL, 2, 2), (Z1, 1, 5), (BL, 2, 0),
+    (Q1, 0, 2, 0), (BL, 0, 3), (Z1, 1, 6), (Q2, 0, 2), (WD, 0),
 )
-CHUNK_STEPS = (
-    (
-        (Q2, 2, 1), (Q2, 2, 2), (Z1, 2, 5), (Q1, 1, 1, 0), (Q1, 1, 1, 1),
-    ),
-    (
-        (Z1, 2, 6), (Q1, 1, 2, 0), (Q1, 1, 2, 1),
-    ),
-    (
-        (Q2, 2, 0), (Q2, 2, 3), (Z2, 2, 1, 0), (Z2, 2, 0, 2), (Q1, 1, 3, 0), (Q1, 1, 3, 1), (Z1, 2, 7),
-    ),
-    (
-        (Z2, 2, 1, 1), (Z2, 2, 1, 2), (Z2, 2, 0, 3),
-    ),
-    (
-        (Q2, 1, 1), (Q2, 1, 2),
-    ),
-    (
-        (Q2, 1, 3), (Z2, 2, 1, 3),
+GATE_STEPS = (
+    (),
+    (
+        (Q2, 1, 0), (Z1, 1, 7), (Z2, 1, 1, 0), (P2, 1, 0), (P2, 1, 1), (CI, 0),
+    ),
+    (
+        (Z2, 1, 0, 1), (Z2, 1, 1, 1), (Z2, 1, 0, 2), (BL, 1, 1), (BL, 2, 3), (Q1, 2, 1, 1), (Q1, 2, 1, 0), (Z2, 1, 1, 2), (Q1, 0, 3, 1),
+        (Z2, 1, 0, 3), (Q1, 2, 2, 0), (Q1, 2, 2, 1), (Q2, 0, 1),
+    ),
+    (
+        (Z2, 1, 1, 3), (Z2, 2, 0, 1), (BL, 1, 2), (Q1, 1, 1, 1), (CI, 1),
+    ),
+    (
+        (Z1, 2, 2), (BL, 1, 3), (Q1, 2, 0, 0), (Q1, 2, 0, 1),
+    ),
+    (
+        (Q1, 0, 3, 0), (Z1, 2, 3), (CI, 2),
+    ),
+    (
+        (Q2, 0, 3), (Z1, 2, 4), (Z1, 2, 5), (Q1, 2, 3, 0), (Q1, 2, 3, 1),
+    ),
+    (
+        (WD, 1), (Q2, 2, 1), (Q2, 2, 2), (Z1, 2, 6), (Q1, 1, 1, 0), (Q1, 1, 2, 1), (CI, 3),
+    ),
+)
+UP_STEPS = (
+    (
+        (Z1, 2, 7), (Q1, 1, 2, 0),
+    ),
+    (
+        (Q2, 2, 0), (Q2, 2, 3), (Z2, 2, 1, 0), (Z2, 2, 0, 2), (Q1, 1, 3, 1),
+    ),
+    (
+        (Z2, 2, 1, 1), (Q1, 1, 3, 0),
+    ),
+    (
+        (Z2, 2, 0, 3), (Q2, 1, 2),
+    ),
+    (
+        (Q2, 1, 1), (Z2, 2, 1, 2),
+    ),
+    (
+        (Z2, 2, 1, 3),
+    ),
+    (
+        (Q2, 1, 3),
     ),
     (),
 )
@@ -58,6 +83,18 @@
     (WD, 2),
 )
 Z_ORDER = (2, 0, 1)
+EARLY_ORDER = (
+    ('far_block', 2), ('next_products', 2),
+)
+LATE_ORDER = (
+    ('next_adds', 2), ('give_rows', 0), ('far_block', 0), ('far_block', 1), ('next_products', 0), ('keep_rows', 0), ('ring_first', 0, 1),
+    ('own_block', 2), ('finish', 2, 1), ('finish', 2, 0), ('finish', 2, 3), ('finish', 2, 4), ('give_rows', 1), ('finish', 2, 2),
+    ('next_adds', 0), ('own_block', 0), ('ring_dependent', 0, 1), ('keep_rows', 1), ('ring_first', 1, 1), ('next_blocks', 1),
+    ('ring_last', 0, 1), ('ring_first', 0, 2), ('own_block', 1), ('finish', 0, 0), ('ring_dependent', 0, 2), ('ring_dependent', 1, 1),
+    ('finish', 0, 1), ('finish', 0, 3), ('ring_last', 0, 2), ('finish', 0, 4), ('finish', 0, 2), ('finish', 1, 0), ('finish', 1, 1),
+    ('ring_last', 1, 1), ('ring_first', 1, 2), ('finish', 1, 2), ('ring_dependent', 1, 2), ('finish', 1, 3), ('finish', 1, 4),
+    ('ring_last', 1, 2),
+)
 
 
 def dot(a, b, ca, cb):
@@ -125,6 +162,11 @@
         for c in copies:
             c.wait_send()
 
+    def run_order(fns, order):
+        for fn, *args in order:
+            with jax.named_scope("_".join(str(v) for v in [fn, *args])):
+                fns[fn](*args)
+
     barrier = pltpu.get_barrier_semaphore()
     others = [zdev(1), zdev(3), ydev(1), ydev(3)] + [near(*n) for n in NEAR[1:]]
     for dev in others:
@@ -134,7 +176,23 @@
         src = tok_all if t < 2 else grad_all
         return pltpu.make_async_copy(src.at[:, pl.ds(lanes_at[k], cols)], blk.at[slot], blk_sem.at[slot])
 
-    def product(t, slot, dst):
+    plan = []
+    for fn, *args in EARLY_ORDER + LATE_ORDER:
+        plan += [(args[0], k) for k in {"far_block": (2,), "next_blocks": (1, 3), "next_products": (1, 3), "own_block": (0,)}.get(fn, ())]
+    taken = []
+
+    def next_block():
+        n = len(taken)
+        taken.append(n)
+        if n == 0:
+            blk_load(plan[0][0], 0, plan[0][1]).start()
+        blk_load(plan[n][0], n % 2, plan[n][1]).wait()
+        if n + 1 < len(plan):
+            blk_load(plan[n + 1][0], (n + 1) % 2, plan[n + 1][1]).start()
+        return n % 2
+
+    def product(t, dst):
+        slot = next_block()
         step = 2 * LANE
 
         def one(n, carry):
@@ -157,10 +215,20 @@
         return [rcopy(nxt.at[t, s, at], rb.at[t, s, at], u_s.at[t, s, tile], u_r.at[t, s, tile], zdev(1 + 2 * s)) for s in range(2)]
 
     def far_block(t):
-        blk_load(t, 0, 2).start()
-        blk_load(t, 0, 2).wait()
-        product(t, 0, far.at[t])
+        product(t, far.at[t])
         start(a_copies(t))
+
+    def early_units(t):
+        if ("next_products", t) not in EARLY_ORDER + LATE_ORDER:
+            return ()
+        free = [(0, tile) for tile in range(tiles) if tile * LANE >= half]
+        return free + [(1, tile) for tile in range(tiles) if (tile + 1) * LANE <= half]
+
+    def next_products(t):
+        for s in range(2):
+            product(t, nxt.at[t, s])
+        for s, tile in early_units(t):
+            unit_copies(t, tile)[s].start()
 
     def forward_phase(shard, pieces, wv, rowbuf, av, bv, hst):
         fulls = (wg, wu, wd)
@@ -297,8 +365,11 @@
             copy(there, there, q2_s.at[r, ia], q2_r.at[r, ia], {"datb": z}).wait_recv()
             to_core(r, ia, 3)
 
-        def rows_in(r):
-            for ia in range(RING):
+        def chunk_in(ia):
+            rows_in(0, (ia,))
+
+        def rows_in(r, blocks=range(RING)):
+            for ia in blocks:
                 for ib in range(RING):
                     there = block(r, DELTAS[ia], DELTAS[ib], 1)
                     copy(there, there, cc_s.at[r, ia, ib], cc_r.at[r, ia, ib], {"datb": z}).wait_recv()
@@ -352,13 +423,28 @@
             for c in range(2):
                 h_copy(RING - 1, c, slot, j).wait()
 
-        def pre_work(i, xx, c):
-            rb_ = rowbuf[c]
-            a = jnp.dot(rb_, wv[0], preferred_element_type=F32).astype(BF16)
-            b = jnp.dot(rb_, wv[1], preferred_element_type=F32).astype(BF16)
-            av[chunk_rows(i)] = a
+        def gate_work():
+            def outer(ia, carry):
+                delta = lax.rem(3 * ia + 3 * lax.div(ia, 2) + 2 * lax.div(ia, 3), RING)
+
+                def inner(flip, carry):
+                    for k, group in enumerate(GATE_STEPS):
+                        if group:
+                            pl.when(2 * ia + flip == k)(functools.partial(run, group))
+                    i = 2 * lax.rem(x + delta, RING) + lax.rem(core + flip, 2)
+                    row_load(tok_all, i, 0).start()
+                    row_load(tok_all, i, 0).wait()
+                    av[chunk_rows(i)] = jnp.dot(rowbuf[0], wv[0], preferred_element_type=F32).astype(BF16)
+                    return carry
+
+                return lax.fori_loop(0, 2, inner, carry)
+
+            lax.fori_loop(0, RING, outer, 0)
+
+        def up_work(i, xx, c):
+            b = jnp.dot(rowbuf[c], wv[1], preferred_element_type=F32).astype(BF16)
             bv[chunk_rows(i)] = b
-            a, b = a.astype(F32), b.astype(F32)
+            a, b = av[chunk_rows(i)].astype(F32), b.astype(F32)
             keep(i, xx, c, 0, 2, a * jax.nn.sigmoid(a) * b)
 
         def post_work(i, xx, c):
@@ -368,7 +454,7 @@
             keep(i, xx, c, 0, 0, g * b * sig * (1.0 + a * (1.0 - sig)))
             keep(i, xx, c, 1, 1, g * (a * sig))
 
-        steps = (exchange, z_first, z_second, first_own, first_forward, block_on, second_forward, second_far, weights_done)
+        steps = (exchange, z_first, z_second, first_own, first_forward, block_on, second_forward, second_far, weights_done, chunk_in)
 
         def run(group):
             for which, *args in group:
@@ -383,17 +469,19 @@
         with jax.named_scope("gather"):
             run(GATHER_STEPS)
             local[3].wait()
-            rows_in(0)
             w_load(0).wait()
+        with jax.named_scope("gate"):
+            gate_work()
+        with jax.named_scope("up"):
+            run(UP_STEPS[0])
             w_load(1).wait()
-        with jax.named_scope("gate_up"):
-            chunk_loop(tok_all, pre_work, [functools.partial(run, group) for group in CHUNK_STEPS])
+            chunk_loop(tok_all, up_work, [functools.partial(run, group) for group in ((),) + UP_STEPS[1:]])
             kept(0, 2)
         with jax.named_scope("rows"):
             for r in (1, 2):
                 local[3 + r].wait()
                 rows_in(r)
-        far_block(2)
+        run_order({"far_block": far_block, "next_products": next_products}, EARLY_ORDER)
         with jax.named_scope("late"):
             run(LATE_STEPS)
             w_load(2).wait()
@@ -405,38 +493,34 @@
             make(*args).wait_send()
 
     def backward_phase(tmp, stage):
+        def next_adds(t):
+            received(a_copies(t))
+            cs = [pltpu.make_async_copy(ra.at[t, at], tmp.at[s, at], tmp_sem.at[s]) for s, at in ((0, lo), (1, hi))]
+            start(cs)
+            for c, (s, at) in zip(cs, ((0, lo), (1, hi))):
+                c.wait()
+                nxt[t, s, at] += tmp[s, at]
+            for tile in range(tiles):
+                start(c for s, c in enumerate(unit_copies(t, tile)) if (s, tile) not in early_units(t))
+
         def next_blocks(t):
-            for s in range(2):
-                blk_load(t, s, 1 + 2 * s).start()
-            for s in range(2):
-                blk_load(t, s, 1 + 2 * s).wait()
-                product(t, s, nxt.at[t, s])
-            received(a_copies(t))
-            cs = [pltpu.make_async_copy(ra.at[t, rows], tmp.at[s, rows], tmp_sem.at[s]) for s, rows in ((0, lo), (1, hi))]
-            start(cs)
-            for c, (s, rows) in zip(cs, ((0, lo), (1, hi))):
-                c.wait()
-                nxt[t, s, rows] += tmp[s, rows]
-            for tile in range(tiles):
-                start(unit_copies(t, tile))
+            next_products(t)
+            next_adds(t)
 
         def own_block(t):
-            blk_load(t, 0, 0).start()
             sent(a_copies(t))
-            blk_load(t, 0, 0).wait()
-            product(t, 0, far.at[t])
+            product(t, far.at[t])
 
         def slot(t):
             return Z_ORDER.index(t) % 2
 
         def hand_out(t, tile):
-            lanes = pl.ds(tile * LANE, LANE)
             cs = []
             for k in range(1, n8):
                 at = pl.ds(hand_at[NEAR[k][0]][NEAR[k][1]], dp)
-                cs.append(rcopy(stage.at[slot(t), at, lanes], outs[t].at[i8, :, lanes], e_s.at[t, tile, k], e_r.at[t, tile, k], near(*NEAR[k])))
+                cs.append(rcopy(stage.at[slot(t), tile, at], outs[t].at[i8, tile], e_s.at[t, tile, k], e_r.at[t, tile, k], near(*NEAR[k])))
             at = pl.ds(hand_at[0][0], dp)
-            return cs, pltpu.make_async_copy(stage.at[slot(t), at, lanes], outs[t].at[i8, :, lanes], out_sem.at[t, tile])
+            return cs, pltpu.make_async_copy(stage.at[slot(t), tile, at], outs[t].at[i8, tile], out_sem.at[t, tile])
 
         def handed(t, tile):
             cs, mine = hand_out(t, tile)
@@ -453,7 +537,7 @@
             for c in cs:
                 c.wait()
             wide = pl.ds(tile * LANE, LANE)
-            stage[slot(t), :, wide] = (far[t, wide] + tmp[0, wide] + tmp[1, wide]).T
+            stage[slot(t), tile] = (far[t, wide] + tmp[0, wide] + tmp[1, wide]).T
             cs, mine = hand_out(t, tile)
             start(cs + [mine])
 
@@ -554,17 +638,11 @@
             core_copy(r).wait_recv()
             row_products(r, True)
 
-        order = [
-            (far_block, 0), (give_rows, 0), (next_blocks, 2), (far_block, 1), (own_block, 2), (keep_rows, 0), (ring_first, 0, 1),
-            (finish, 2, 0), (give_rows, 1), (finish, 2, 1), (finish, 2, 2), (next_blocks, 0), (finish, 2, 3), (ring_dependent, 0, 1),
-            (finish, 2, 4), (own_block, 0), (keep_rows, 1), (ring_first, 1, 1), (next_blocks, 1), (ring_last, 0, 1), (ring_first, 0, 2),
-            (finish, 0, 0), (own_block, 1), (finish, 0, 1), (ring_dependent, 0, 2), (ring_dependent, 1, 1), (finish, 0, 2), (finish, 0, 3),
-            (ring_last, 0, 2), (finish, 0, 4), (finish, 1, 0), (finish, 1, 1), (ring_last, 1, 1), (ring_first, 1, 2), (finish, 1, 2),
-            (ring_dependent, 1, 2), (finish, 1, 3), (finish, 1, 4), (ring_last, 1, 2),
-        ]
-        for fn, *args in order:
-            with jax.named_scope("_".join(str(v) for v in [fn.__name__, *args])):
-                fn(*args)
+        run_order({
+            "far_block": far_block, "next_products": next_products, "next_adds": next_adds, "next_blocks": next_blocks,
+            "own_block": own_block, "finish": finish, "give_rows": give_rows, "keep_rows": keep_rows, "ring_first": ring_first,
+            "ring_dependent": ring_dependent, "ring_last": ring_last,
+        }, LATE_ORDER)
 
         for t in range(3):
             for tile in range(tiles):
@@ -587,7 +665,7 @@
         pltpu.VMEM((tokens, nf), BF16),
         pltpu.VMEM((2, 2, chunk, nf), BF16),
     )
-    pl.run_scoped(backward_phase, pltpu.VMEM((2, tiles * LANE, cols), F32), pltpu.VMEM((2, cols, tiles * LANE), F32))
+    pl.run_scoped(backward_phase, pltpu.VMEM((2, tiles * LANE, cols), F32), pltpu.VMEM((2, tiles, cols, LANE), F32))
 
 
 def layer(sg, su, sd, tok, grad):
@@ -604,7 +682,7 @@
     halves = (2, rows // 2, d)
     res = pl.pallas_call(
         layer_kernel,
-        out_shape=[sds((n8, dp, padded), F32)] * 3 + [sds(halves, BF16)] * 2 + [
+        out_shape=[sds((n8, tiles, dp, LANE), F32)] * 3 + [sds(halves, BF16)] * 2 + [
             sds((d, nf), BF16), sds((d, nf), BF16), sds((d, nf), BF16), sds((tokens, d), BF16), sds((tokens, d), BF16),
             sds((3, RING, 2, RING * rows, nf), BF16),
             sds((3, nf, cols), F32), sds((3, 2, nf, cols), F32),
@@ -654,7 +732,7 @@
     for t in range(3):
         loads[t].wait()
         for j in range(n8):
-            flat[t, :, j * nf:(j + 1) * nf] = buf[t, j, :, :nf]
+            flat[t, :, j * nf:(j + 1) * nf] = jnp.concatenate([buf[t, j, tile] for tile in range(buf.shape[2])], axis=1)[:, :nf]
         stores[t].start()
     rows_out = [pltpu.make_async_copy(row_buf.at[r], dst, row_sem.at[r]) for r, dst in enumerate((res, gres))]
     for c in rows_in:
@@ -666,7 +744,7 @@
 
 
 def assemble(sums, out, gin, ff):
-    n8, dp, padded = sums[0].shape
+    dp = sums[0].shape[2]
     hbm = pl.BlockSpec(memory_space=pl.ANY)
     dma = pltpu.SemaphoreType.DMA
     sds = jax.ShapeDtypeStruct
@@ -676,7 +754,7 @@
         in_specs=[hbm] * 5,
         out_specs=[hbm] * 5,
         scratch_shapes=[
-            pltpu.VMEM((3, n8, dp, padded), F32), pltpu.VMEM((3, dp, ff), F32), dma((3,)), dma((3,)),
+            pltpu.VMEM((3,) + sums[0].shape, F32), pltpu.VMEM((3, dp, ff), F32), dma((3,)), dma((3,)),
             pltpu.VMEM((2,) + out.shape, BF16), dma((2,)),
         ],
         compiler_params=pltpu.CompilerParams(vmem_limit_bytes=63 * 1024 * 1024),

time: 369 us -> 359 us (0.973)
  Pallas kernels: 366 us -> 356 us
    pallas_call x1, Pallas kernels: 361 us -> 351 us  [layer(): pl.pallas_call(layer_kernel, out_shape=[sds((n8, tiles, dp, LANE), F32)]...]
where the time goes in v3:
time: 359 us; the launch traced here: 357 us
  Pallas kernels  356 us (99%)
    pallas_call x1, Pallas kernels, layer(): pl.pallas_call(layer_kernel, out_shape=[sds((n8, tiles, dp, LANE), F32)]...  351 us

profile of v3, /device:TPU:1, one launch (start us, length us, event | category | flops | bytes accessed | tf_op | source)
XLA Modules:
  0.0 357.0 jit_solution(4958460193594233394)
XLA Ops:
  0.6 350.8 %layer.1 = (f32[8,5,112,128]{3,2,1,0:T(8,128)}, f32[8,5,112,128]{3,2,1,0:T(8,128)}, f32[8,5,112,128]{3,2,1,0:T(8,128)}, bf16[2,32,3584]{2,1,0:T(8,128)(2,1)}, bf...) custom-call(bf16[112,4736]{1,0:T(8,128)(2,1)} %sg.1, ...), custom_call_target="tpu_custom_call" | custom-call | flops 78215380992 | bytes 300000000 | tf_op jit(solution)/shard_map/layer/pallas_call | solution.py:683
  351.4 5.4 %assemble.1 = (f32[112,4736]{1,0:T(8,128)}, f32[112,4736]{1,0:T(8,128)}, f32[112,4736]{1,0:T(8,128)}, bf16[64,3584]{1,0:T(8,128)(2,1)}, bf16[64,3584]{1,0:T(8,128)(2,1)}) custom-call(f32[8,5,112,128]{3,2,1,0:T(8,128)} %get-tuple-element.15.og, f32[8,5,112,128]{3,2,1,0:T(8,128)} %get-tuple-element.16.ou, f32[8,5,112,128]{3,2,1,0:T(8,128)} %get-tuple-element.17.od, ...), custom_call_target="tpu_custom_call" | custom-call | tf_op jit(solution)/shard_map/assemble/pallas_call | solution.py:751
